TPU v7x, 512 devices: a 8x2x16 block of a 8x8x16 slice. The times are simulated.
512 devices in a mesh: groups: 2 (over y), seq: 16 (over z), tensor: 8 (over x), sub: 2 (over core).
Axes of the slice: x: 8, y: 2, z: 16, core: 2. Of those that a mesh axis runs over, the one named last changes fastest.
The devices are a block of a 8x8x16 slice.
Arguments:
- image_tokens: bfloat16 [8192, 3072], P(('groups', 'seq')), parts along dimension 0, may hold values from -6 to 6
- text_tokens: bfloat16 [1024, 3072], P(('groups', 'seq')), parts along dimension 0, may hold values from -6 to 6
- timestep: int32 [2], P('groups'), parts along dimension 0, may hold values from 0 to 49
- text_length: int32 [2], P('groups'), parts along dimension 0, may hold values from 128 to 512
- time_table: bfloat16 [50, 3072], replicated, may hold values from -6 to 6
- mod_weight: bfloat16 [3072, 18432], P('seq', ('tensor', 'sub')), may hold values from -0.109375 to 0.109375
- qkv_image: bfloat16 [3072, 6144], P('seq', ('tensor', 'sub')), as said below
- qkv_text: bfloat16 [3072, 6144], P('seq', ('tensor', 'sub')), as said below
- norm_gain: float32 [2, 2, 16, 128], P(None, None, ('tensor', 'sub')), may hold values from 1 to 6
- proj_image: bfloat16 [2048, 3072], P(('tensor', 'sub'), 'seq'), may hold values from -0.125 to 0.125
- proj_text: bfloat16 [2048, 3072], P(('tensor', 'sub'), 'seq'), may hold values from -0.125 to 0.125
Outputs:
- image_out: bfloat16 [8192, 3072], P(('groups', 'seq'), ('tensor', 'sub')), parts along dimension 0
- text_out: bfloat16 [1024, 3072], P(('groups', 'seq'), ('tensor', 'sub')), parts along dimension 0
There are 2 independent parts, one for each index of `groups`. A program takes and returns all parts, laid end to end along the dimension named above; an argument that names none is the same for every part. Nothing has to cross between parts.
Inputs may be any that keep to these rules, and one draw needn't show every extreme that they name: `qkv_image`: entries of standard deviation about 1/sqrt(3072). `qkv_text`: entries of standard deviation about 1/sqrt(3072).
All inputs are finite; a program needn't handle non-finite values.
Results may differ from a plain program's by a relative error of at most 0.0085.
Values may be sent and summed in bfloat16 or wider, within the bound.
A program may use at most 64 MiB of HBM per device.

v0:
```python
import jax
import jax.numpy as jnp
from jax import lax
from jax.sharding import PartitionSpec as P

EPSILON = 1e-06


def copy_for_each(x, axis):
    copies = jnp.broadcast_to(x, (lax.axis_size(axis), *x.shape))
    return lax.all_to_all(copies, axis, split_axis=0, concat_axis=0, tiled=True)


def over_copies(x, axis):
    everything = copy_for_each(x, axis)
    return jnp.sum(everything, axis=0)


def side_by_side(arrays, axis, dim, along):
    ends, at = ([], 0)
    for a in arrays[:-1]:
        at += a.shape[along]
        ends.append(at)
    both = jnp.concatenate(arrays, axis=along)
    return tuple(jnp.split(lax.all_gather(both, axis, axis=dim, tiled=True), ends, axis=along))


def joined_along(tiles, dim):
    shape = list(tiles.shape[1:])
    shape[dim] *= tiles.shape[0]
    return jnp.moveaxis(tiles, 0, dim).reshape(shape)


def gather_directly(x, axis, dim):
    return joined_along(copy_for_each(x, axis), dim)


def modulate(tokens, shift, scaling):
    values = tokens.astype(jnp.float32)
    center = jnp.mean(values, axis=-1, keepdims=True)
    spread = jnp.mean(jnp.square(values - center), axis=-1, keepdims=True)
    normed = (values - center) * lax.rsqrt(spread + EPSILON)
    return (normed * (1.0 + scaling) + shift).astype(jnp.bfloat16)


def head_norm(values, gain):
    return values * lax.rsqrt(jnp.mean(values * values, axis=-1, keepdims=True) + EPSILON) * gain


def split_heads(projected, gains):
    shaped = projected.reshape(projected.shape[0], -1, 3, gains.shape[-1])
    queries = head_norm(shaped[:, :, 0], gains[0]).astype(jnp.bfloat16)
    keys = head_norm(shaped[:, :, 1], gains[1]).astype(jnp.bfloat16)
    values = shaped[:, :, 2].astype(jnp.bfloat16)
    return (queries, keys, values)


def add_rows(source, shards):
    return jnp.dot(source, shards, preferred_element_type=jnp.float32)


def body(
    image_tokens,
    text_tokens,
    timestep,
    text_length,
    time_table,
    mod_weight,
    qkv_image,
    qkv_text,
    norm_gain,
    proj_image,
    proj_text,
):
    columns_all = image_tokens.shape[1]
    embedded = lax.dynamic_index_in_dim(time_table, timestep[0], 0, keepdims=False).astype(
        jnp.float32
    )
    vector = jax.nn.silu(embedded).astype(jnp.bfloat16)
    slab_rows = mod_weight.shape[0]
    vector_rows = lax.dynamic_slice_in_dim(vector, lax.axis_index("seq") * slab_rows, slab_rows)
    partial_value = jnp.dot(vector_rows[None, :], mod_weight, preferred_element_type=jnp.float32)[0]
    summed_rows = over_copies(partial_value, "seq")
    modulation = lax.all_gather(summed_rows, ("tensor", "sub"), axis=0, tiled=True)
    modulation = modulation.reshape(2, 3, columns_all)
    hidden_image = modulate(image_tokens, modulation[0, 0], modulation[0, 1])
    hidden_text = modulate(text_tokens, modulation[1, 0], modulation[1, 1])
    image_count = image_tokens.shape[0]
    text_count = text_tokens.shape[0]
    local_rows = image_count + text_count
    shards = side_by_side((qkv_image, qkv_text), "seq", 0, 1)
    projected_image = add_rows(hidden_image, shards[0])
    projected_text = add_rows(hidden_text, shards[1])
    image_q, image_k, image_v = split_heads(projected_image, norm_gain[0])
    text_q, text_k, text_v = split_heads(projected_text, norm_gain[1])
    heads_here = image_q.shape[1]
    head_size = image_q.shape[2]
    queries = jnp.concatenate([text_q, image_q], axis=0)
    keys = jnp.concatenate([text_k, image_k], axis=0)
    values = jnp.concatenate([text_v, image_v], axis=0)
    keys_values = jnp.stack([keys, values], axis=2).reshape(local_rows, heads_here * 2 * head_size)
    factor = float(head_size) ** (-0.5)
    shards = lax.all_gather(keys_values, "seq", axis=0, tiled=True)
    count = shards.shape[0]
    blocks = shards.reshape(count, heads_here, 2, head_size)
    position = jnp.arange(count, dtype=jnp.int32)
    within = position % local_rows
    owner = position // local_rows
    usable = (within >= text_count) | (owner * text_count + within < text_length[0])
    scores = (
        jnp.einsum("qhd,khd->hqk", queries, blocks[:, :, 0], preferred_element_type=jnp.float32)
        * factor
    )
    scores = jnp.where(usable[None, None, :], scores, -1e30)
    run_max = jnp.full((heads_here, local_rows), -1e30, jnp.float32)
    new_max = jnp.maximum(run_max, jnp.max(scores, axis=-1))
    probs = jnp.exp(scores - new_max[:, :, None])
    run_sum = jnp.sum(probs, axis=-1)
    totals = jnp.einsum(
        "hqk,khd->hqd",
        probs.astype(jnp.bfloat16),
        blocks[:, :, 1],
        preferred_element_type=jnp.float32,
    )
    final_max, run_sum, totals = (new_max, run_sum, totals)
    attended = (
        (totals / run_sum[:, :, None])
        .astype(jnp.bfloat16)
        .transpose(1, 0, 2)
        .reshape(local_rows, heads_here * head_size)
    )
    stacked = jnp.stack([proj_image, proj_text], axis=0)
    width_here = columns_all // lax.axis_size(("tensor", "sub"))
    first = lax.axis_index(("tensor", "sub")) * width_here
    attended_all = lax.all_gather(attended, ("tensor", "sub"), axis=1, tiled=True)
    full_columns = gather_directly(stacked, "seq", 2)
    all_rows = lax.all_to_all(
        full_columns, ("tensor", "sub"), split_axis=2, concat_axis=1, tiled=True
    )
    text_part = jnp.dot(attended_all[:text_count], all_rows[1], preferred_element_type=jnp.float32)
    image_part = jnp.dot(attended_all[text_count:], all_rows[0], preferred_element_type=jnp.float32)
    summed = jnp.concatenate([text_part, image_part], axis=0)
    gates = lax.dynamic_slice_in_dim(modulation[:, 2], first, width_here, 1)
    image_base = lax.dynamic_slice_in_dim(image_tokens, first, width_here, 1).astype(jnp.float32)
    text_base = lax.dynamic_slice_in_dim(text_tokens, first, width_here, 1).astype(jnp.float32)
    image_out = (image_base + gates[0] * summed[text_count:]).astype(jnp.bfloat16)
    text_out = (text_base + gates[1] * summed[:text_count]).astype(jnp.bfloat16)
    return (image_out, text_out)


def solution(mesh):
    return jax.shard_map(
        body,
        mesh=mesh,
        in_specs=(
            P(("groups", "seq"), None),
            P(("groups", "seq"), None),
            P("groups"),
            P("groups"),
            P(),
            P("seq", ("tensor", "sub")),
            P("seq", ("tensor", "sub")),
            P("seq", ("tensor", "sub")),
            P(None, None, ("tensor", "sub"), None),
            P(("tensor", "sub"), "seq"),
            P(("tensor", "sub"), "seq"),
        ),
        out_specs=(
            P(("groups", "seq"), ("tensor", "sub")),
            P(("groups", "seq"), ("tensor", "sub")),
        ),
        check_vma=False,
    )
```

profile of v0, /device:TPU:65, one launch (start us, length us, event | category | flops | bytes accessed | tf_op | source)
XLA Modules:
  0.0 331.8 jit_solution(2012975773529519492)
XLA Ops:
  7.3 1.8 pad_maximum_fusion
  11.6 44.2 %all-to-all-start = ((f32[16,1,1152]{2,1,0:T(1,128)}), f32[16,1,1152]{2,1,0:T(1,128)S(1)}, u32[]{:S(2)}, u32[]{:S(2)}) async-start(f32[16,1,1152]{2,1,0:T(1,128)} %broadcast_in_dim.14), calls=%async_computation | async-start | bytes 147456 | tf_op jit(solution)/shard_map/all_to_all | solution.py:11
  55.9 1.1 convert_reduce_fusion.1
  56.9 1.2 fusion.38
  59.1 8.3 %all-to-all-done = f32[16,1,1152]{2,1,0:T(1,128)S(1)} async-done(((f32[16,1,1152]{2,1,0:T(1,128)}), f32[16,1,1152]{2,1,0:T(1,128)S(1)}, u32[]{:S(2)}, u32[]{:S(2)}) %all-to-all-start) | async-done | bytes 73760 | tf_op jit(solution)/shard_map/all_to_all | solution.py:11
  67.4 1.5 broadcast_in_dim.22
  68.9 4.8 %all-to-all-start.1 = ((bf16[16,2,128,192]{2,3,1,0:T(8,128)(2,1)}), bf16[16,2,128,192]{2,3,1,0:T(8,128)(2,1)}, u32[]{:S(2)}, u32[]{:S(2)}) async-start(bf16[16,2,128,192]{2,3,1,0:T(8,128)(2,1)} %broadcast_in_dim.22), calls=%async_computation.1 | async-start | bytes 3145728 | tf_op jit(solution)/shard_map/all_to_all | solution.py:11
  73.8 20.3 %all-gather = f32[16,1,1152]{2,1,0:T(1,128)S(1)} all-gather(f32[1,1,1152]{2,1,0:T(1,128)S(1)} %reshape.562), channel_id=1, replica_groups=mesh['groups'=2,'seq'=16,'tensor'=8,'sub'=2] {'tensor','sub'}, dimensions={0}, use_global_device_ids=true | all-gather | bytes 78336 | tf_op jit(solution)/shard_map/all_gather | solution.py:84
  94.4 90.3 %all-gather.5.cloned.1.call-done = bf16[3072,768]{1,0:T(8,128)(2,1)} async-done(((bf16[192,768]{1,0:T(8,128)(2,1)}), bf16[3072,768]{1,0:T(8,128)(2,1)}) %all-gather.5.cloned.1.call-update) | async-done | bytes 4718608 | tf_op jit(solution)/shard_map/all_gather | solution.py:25
  184.7 2.2 fusion.14
  187.4 3.0 fusion.12
  192.3 1.5 copy.69
  193.9 13.8 %copy.70 = bf16[2,128,3072]{1,0,2:T(2,128)(2,1)} copy(bf16[2,128,3072]{1,2,0:T(8,128)(2,1)S(1)} %bitcast.86) | data formatting | bytes 3145728 | tf_op jit(solution)/shard_map/reshape | solution.py:31
  207.7 13.5 %all-to-all-start.2 = ((bf16[2,128,3072]{1,0,2:T(2,128)(2,1)}), bf16[2,128,3072]{1,0,2:T(2,128)(2,1)}, u32[]{:S(2)}, u32[]{:S(2)}) async-start(bf16[2,128,3072]{1,0,2:T(2,128)(2,1)} %copy.70), calls=%async_computation.2 | async-start | bytes 3145728 | tf_op jit(solution)/shard_map/all_to_all | solution.py:137
  221.7 38.3 %all-gather.7.cloned.1.call-done = bf16[4608,256]{1,0:T(8,128)(2,1)} async-done(((bf16[288,256]{1,0:T(8,128)(2,1)}), bf16[4608,256]{1,0:T(8,128)(2,1)}) %all-gather.7.cloned.1.call-update) | async-done | bytes 2359312 | tf_op jit(solution)/shard_map/all_gather | solution.py:103
  260.0 4.6 %reshape.557 = bf16[4608,1,2,128]{3,2,0,1:T(2,128)(2,1)S(1)} reshape(bf16[4608,256]{1,0:T(8,128)(2,1)} %all-gather.7.cloned.1.call-done) | data formatting | bytes 4718592 | tf_op jit(solution)/shard_map/reshape | solution.py:105
  264.7 3.4 %fusion.63 = (bf16[4608,1,1,128]{3,2,0,1:T(2,128)(2,1)S(1)}, bf16[4608,1,1,128]{3,2,0,1:T(2,128)(2,1)S(1)}) fusion(bf16[4608,1,2,128]{3,2,0,1:T(2,128)(2,1)S(1)} %reshape.557), kind=kLoop, calls=%fused_computation.110 | loop fusion | bytes 4718592 | tf_op jit(solution)/shard_map/slice | solution.py:111
  268.1 1.3 fusion.66
  270.2 1.6 fusion.28
  271.8 1.0 constant_dynamic-slice_fusion.2
  273.1 1.6 copy.71
  275.9 45.1 %all-gather.9.cloned.1.call-done = bf16[288,2048]{1,0:T(8,128)(2,1)} async-done(((bf16[288,128]{1,0:T(8,128)(2,1)}), bf16[288,2048]{1,0:T(8,128)(2,1)}) %all-gather.9.cloned.1.call-update) | async-done | bytes 1179664 | tf_op jit(solution)/shard_map/all_gather | solution.py:135
  321.0 1.9 fusion.24
  322.9 2.4 fusion.22
  (67 shorter events, 7.8 us)
Async XLA Ops:
  7.2 3.6 %copy-start = (bf16[192,1152]{1,0:T(8,128)(2,1)S(1)}, bf16[192,1152]{1,0:T(8,128)(2,1)}, u32[]{:S(2)}) copy-start(bf16[192,1152]{1,0:T(8,128)(2,1)} %param.16) | copy-start | bytes 1327108
  7.2 50.9 %copy-start.1 = (bf16[256,3072]{1,0:T(8,128)(2,1)S(1)}, bf16[256,3072]{1,0:T(8,128)(2,1)}, u32[]{:S(2)}) copy-start(bf16[256,3072]{1,0:T(8,128)(2,1)} %param.11) | copy-start | bytes 4718596
  7.2 177.5 %all-gather.5.cloned.1.call-start = ((), (), s32[]{:S(2)}) async-start(), calls=%async_computation.3 | async-start | bytes 5013504 | tf_op jit(solution)/shard_map/all_gather | solution.py:25
  9.1 49.9 %copy-start.3 = (bf16[128,192]{0,1:T(8,128)(2,1)S(1)}, bf16[128,192]{0,1:T(8,128)(2,1)}, u32[]{:S(2)}) copy-start(bf16[128,192]{0,1:T(8,128)(2,1)} %param.21) | copy-start | bytes 147460
  9.1 49.9 %copy-start.4 = (bf16[128,192]{0,1:T(8,128)(2,1)S(1)}, bf16[128,192]{0,1:T(8,128)(2,1)}, u32[]{:S(2)}) copy-start(bf16[128,192]{0,1:T(8,128)(2,1)} %param.20) | copy-start | bytes 147460
  9.1 49.9 %copy-start.5 = (f32[2,2,1,128]{3,2,1,0:T(1,128)S(1)}, f32[2,2,1,128]{3,2,1,0:T(1,128)}, u32[]{:S(2)}) copy-start(f32[2,2,1,128]{3,2,1,0:T(1,128)} %param.19) | copy-start | bytes 6148
  11.6 55.7 %all-to-all-start = ((f32[16,1,1152]{2,1,0:T(1,128)}), f32[16,1,1152]{2,1,0:T(1,128)S(1)}, u32[]{:S(2)}, u32[]{:S(2)}) async-start(f32[16,1,1152]{2,1,0:T(1,128)} %broadcast_in_dim.14), calls=%async_computation | async-start | bytes 147456 | tf_op jit(solution)/shard_map/all_to_all | solution.py:11
  59.0 125.6 %copy-start.2 = (bf16[32,3072]{1,0:T(8,128)(2,1)S(1)}, bf16[32,3072]{1,0:T(8,128)(2,1)}, u32[]{:S(2)}) copy-start(bf16[32,3072]{1,0:T(8,128)(2,1)} %param.12) | copy-start | bytes 589828
  68.9 123.5 %all-to-all-start.1 = ((bf16[16,2,128,192]{2,3,1,0:T(8,128)(2,1)}), bf16[16,2,128,192]{2,3,1,0:T(8,128)(2,1)}, u32[]{:S(2)}, u32[]{:S(2)}) async-start(bf16[16,2,128,192]{2,3,1,0:T(8,128)(2,1)} %broadcast_in_dim.22), calls=%async_computation.1 | async-start | bytes 3145728 | tf_op jit(solution)/shard_map/all_to_all | solution.py:11
  73.7 186.4 %all-gather.7.cloned.1.call-start = ((), (), s32[]{:S(2)}) async-start(), calls=%async_computation.4 | async-start | bytes 2506752 | tf_op jit(solution)/shard_map/all_gather | solution.py:103
  207.7 65.4 %all-to-all-start.2 = ((bf16[2,128,3072]{1,0,2:T(2,128)(2,1)}), bf16[2,128,3072]{1,0,2:T(2,128)(2,1)}, u32[]{:S(2)}, u32[]{:S(2)}) async-start(bf16[2,128,3072]{1,0,2:T(2,128)(2,1)} %copy.70), calls=%async_computation.2 | async-start | bytes 3145728 | tf_op jit(solution)/shard_map/all_to_all | solution.py:137
  221.2 99.8 %all-gather.9.cloned.1.call-start = ((), (), s32[]{:S(2)}) async-start(), calls=%async_computation.5 | async-start | bytes 1253376 | tf_op jit(solution)/shard_map/all_gather | solution.py:135
Sparse Core Ops, SparseCore 0:
  10.1 174.5 all-gather.4
  191.8 68.2 all-gather.6
  271.9 49.0 all-gather.8
where the time goes:
time: 333 us; the launch traced here: 332 us
  waiting for transfers between devices  182 us (55%)
  starting transfers between devices  62.9 us (19%)
  local copies, waits for them, and re-layouts  30.8 us (9%)
  blocking collectives  20.3 us (6%)
  between operations  15.4 us (5%)
  matrix products  12.4 us (4%)
  other arithmetic  7.8 us (2%)
    all_gather x1, waiting for transfers between devices, side_by_side(): lax.all_gather(both, axis, axis=dim, tiled=True)  90.3 us
    all_to_all x2, starting transfers between devices, copy_for_each(): return lax.all_to_all(copies, axis, split_axis=0, concat_axis=0, tiled=True)  49 us
    all_gather x1, waiting for transfers between devices, body(): lax.all_gather(attended, ('tensor', 'sub'), axis=1, tiled=True)  45.1 us
    all_gather x1, waiting for transfers between devices, body(): shards = lax.all_gather(keys_values, 'seq', axis=0, tiled=True)  38.3 us
    all_gather x1, blocking collectives, body(): lax.all_gather(summed_rows, ('tensor', 'sub'), axis=0, tiled=True)  20.3 us
    reshape x1, local copies, waits for them, and re-layouts, joined_along(): return jnp.moveaxis(tiles, 0, dim).reshape(shape)  13.8 us
    all_to_all x1, starting transfers between devices, body(): lax.all_to_all(full_columns, ('tensor', 'sub'), split_axis=2, concat_axis...  13.5 us
    all_to_all x2, waiting for transfers between devices, copy_for_each(): return lax.all_to_all(copies, axis, split_axis=0, concat_axis=0, tiled=True)  8.32 us
  transfers between devices with their start and end apart: 6, of which 4 were waited for; matrix products, arithmetic and copies ran while one was open for 14% of the time, Pallas kernels for 0%

commit v1 on v0

v1 whole, which is shorter than its diff:
```python
import functools
import math

import jax
import jax.numpy as jnp
from jax import lax
from jax.experimental import pallas as pl
from jax.experimental.pallas import tpu as pltpu
from jax.sharding import PartitionSpec as P

EPSILON = 1e-06
MESH = pl.DeviceIdType.MESH
BF16 = jnp.bfloat16
F32 = jnp.float32
RIGHT, LEFT = 0, 1


def rows_at(start, size, unit=16):
    if isinstance(start, int):
        return pl.ds(start, size)
    return pl.ds(pl.multiple_of(start, unit), size)


def cut_three(rows, unit, own):
    third = -(-rows // (3 * unit)) * unit
    rest = rows - 2 * third
    return (own * third, third), (2 * third, rest), ((1 - own) * third, third)


def kernel(
    sizes,
    paired,
    text_length,
    vector_rows,
    image_tokens,
    text_tokens,
    mod_weight,
    norm_gain,
    qkv_image,
    qkv_text,
    proj_image,
    proj_text,
    image_out,
    text_out,
    mod_z,
    mod_all,
    mean_of,
    rstd_of,
    hidden_image,
    hidden_text,
    weights,
    sum_image,
    sum_text,
    proj_z,
    proj_all,
    query,
    key_value,
    row_max,
    row_sum,
    mixed,
    attended,
    load_sem,
    modz_sems,
    modx_sems,
    w_sems,
    wy_sems,
    p_sems,
    py_sems,
    px_sems,
    kv_sems,
    ax_sems,
    as_sems,
):
    nz, nx, nc = sizes
    heads = nx * nc
    z = lax.axis_index("seq")
    x = lax.axis_index("tensor")
    c = lax.axis_index("sub")
    me = x * nc + c
    own = lax.rem(lax.axis_index("groups"), 2) if paired else 0
    other_group = lax.axis_index("groups") + 1 - 2 * own if paired else 0
    image_rows, width = image_tokens.shape
    text_rows = text_tokens.shape[0]
    local_rows = image_rows + text_rows
    slab = qkv_image.shape[0]
    columns = qkv_image.shape[1]
    size = columns // 3
    started = []

    def wrap(i, n):
        return lax.rem(i + n, n)

    def send(src, dst, sems, index, device):
        copy = pltpu.make_async_remote_copy(
            src_ref=src,
            dst_ref=dst,
            send_sem=sems.at[(0, *index)],
            recv_sem=sems.at[(1, *index)],
            device_id=device,
            device_id_type=MESH,
        )
        copy.start()
        started.append(copy)

    def arrive(ref, sems, index, device):
        pltpu.make_async_remote_copy(
            src_ref=ref,
            dst_ref=ref,
            send_sem=sems.at[(0, *index)],
            recv_sem=sems.at[(1, *index)],
            device_id=device,
            device_id_type=MESH,
        ).wait_recv()

    right, left = {"seq": wrap(z + 1, nz)}, {"seq": wrap(z - 1, nz)}
    partner = {"groups": other_group}
    sibling = {"sub": 1 - c}

    loads = [
        pltpu.make_async_copy(qkv_image, weights.at[z, :, pl.ds(0, columns)], load_sem.at[0]),
        pltpu.make_async_copy(qkv_text, weights.at[z, :, pl.ds(columns, columns)], load_sem.at[1]),
        pltpu.make_async_copy(proj_image, proj_z.at[z, 0], load_sem.at[2]),
        pltpu.make_async_copy(proj_text, proj_z.at[z, 1], load_sem.at[3]),
    ]
    for copy in loads:
        copy.start()

    barrier = pltpu.get_barrier_semaphore()
    peers = [{"seq": wrap(z + i, nz)} for i in range(1, nz)]
    plane = [
        {"tensor": lax.div(wrap(me + i, heads), nc), "sub": lax.rem(wrap(me + i, heads), nc)}
        for i in range(1, heads)
    ]
    greeted = peers + plane + ([partner] if paired else [])
    for device in greeted:
        pl.semaphore_signal(barrier, inc=1, device_id=device, device_id_type=MESH)

    mod_z[z] = jnp.dot(vector_rows[...], mod_weight[...], preferred_element_type=F32)

    chunk = 16

    def statistics(tokens, at):
        def one(i, carry):
            rows = rows_at(i * chunk, chunk)
            values = tokens[rows, :].astype(F32)
            center = jnp.mean(values, axis=-1, keepdims=True)
            spread = jnp.mean(jnp.square(values - center), axis=-1, keepdims=True)
            out = rows_at(at + i * chunk, chunk)
            mean_of[out, :] = jnp.broadcast_to(center, (chunk, 128))
            rstd_of[out, :] = jnp.broadcast_to(lax.rsqrt(spread + EPSILON), (chunk, 128))
            return carry

        lax.fori_loop(0, tokens.shape[0] // chunk, one, 0)

    for copy in loads:
        copy.wait()
    pl.semaphore_wait(barrier, len(greeted))

    for i in range(1, nz):
        send(mod_z.at[z], mod_z.at[z], modz_sems, (z,) if False else (i,), {"seq": wrap(z + i, nz)})

    half = nz // 2

    def slab_of(way, d):
        return wrap(z - d, nz) if way == RIGHT else wrap(z + d, nz)

    def parts_at(way, d):
        if d < half:
            return (0, 1)
        return (0,) if way == RIGHT else (1,)

    def ring_step(d, part_ref, sems):
        for way, to in ((RIGHT, right), (LEFT, left)):
            block = slab_of(way, d)
            for part in parts_at(way, d):
                if d > 0:
                    arrive(part_ref(block, part), sems, (way, d, part), to)
                if d < half and part in parts_at(way, d + 1):
                    send(part_ref(block, part), part_ref(block, part), sems, (way, d + 1, part), to)

    def pair_send(d, part_ref, sems):
        if not paired:
            return
        for way in (RIGHT, LEFT):
            if 0 in parts_at(way, d):
                block = slab_of(way, d)
                send(part_ref(block, 0), part_ref(block, 0), sems, (way, d), partner)

    def pair_wait(d, part_ref, sems):
        if not paired:
            return
        for way in (RIGHT, LEFT):
            if 0 in parts_at(way, d):
                arrive(part_ref(slab_of(way, d), 2), sems, (way, d), partner)

    if paired:
        w_parts = cut_three(slab, 16, own)
        p_parts = cut_three(size, 16, own)
    else:
        w_parts = ((0, slab // 2), (slab // 2, slab // 2))
        p_parts = ((0, size // 2), (size // 2, size // 2))

    def w_part(block, part):
        start, count = w_parts[part]
        return weights.at[block, rows_at(start, count), :]

    def p_part(block, part):
        start, count = p_parts[part]
        return proj_z.at[block, :, rows_at(start, count), :]

    ring_step(0, w_part, w_sems)

    statistics(text_tokens, 0)
    statistics(image_tokens, text_rows)

    def mod_over_seq():
        for i in range(1, nz):
            source = wrap(z - i, nz)
            arrive(mod_z.at[source], modz_sems, (i,), {"seq": source})
        total = mod_z[0]
        for i in range(1, nz):
            total = total + mod_z[i]
        mod_all[me] = total
        for i in range(1, heads):
            send(mod_all.at[me], mod_all.at[me], modx_sems, (i,), plane[i - 1])

    def mod_over_plane():
        for i in range(1, heads):
            source = wrap(me - i, heads)
            arrive(mod_all.at[source], modx_sems, (i,), plane[i - 1])

    piece = 2 * slab
    per_block = mod_weight.shape[1] // piece
    pieces = width // piece

    def mod_piece(index):
        if isinstance(index, int):
            return mod_all[index // per_block, :, pl.ds(index % per_block * piece, piece)]
        offset = pl.multiple_of(lax.rem(index, per_block) * piece, 128)
        return mod_all[lax.div(index, per_block), :, pl.ds(offset, piece)]

    def hide(tokens, hidden, stream, at):
        def one(i, carry):
            rows = rows_at(i * chunk, chunk)
            out = rows_at(at + i * chunk, chunk)
            center, scale = mean_of[out, 0:1], rstd_of[out, 0:1]
            for p in range(pieces):
                shift = mod_piece((stream * 3) * pieces + p)
                scaling = mod_piece((stream * 3 + 1) * pieces + p)
                values = tokens[rows, p * piece : (p + 1) * piece].astype(F32)
                values = ((values - center) * scale * (1.0 + scaling) + shift).astype(BF16)
                hidden[2 * p, rows, :] = values[:, :slab]
                hidden[2 * p + 1, rows, :] = values[:, slab:]
            return carry

        lax.fori_loop(0, tokens.shape[0] // chunk, one, 0)

    sum_image[...] = jnp.zeros_like(sum_image)
    sum_text[...] = jnp.zeros_like(sum_text)

    def project(first, last):
        def one(j, carry):
            step = lax.div(j + 1, 2)
            block = wrap(jnp.where(lax.rem(j, 2) == 1, z - step, z + step), nz)
            sum_image[...] += jnp.dot(
                hidden_image[block], weights[block, :, 0:columns], preferred_element_type=F32
            )
            sum_text[...] += jnp.dot(
                hidden_text[block],
                weights[block, :, columns : 2 * columns],
                preferred_element_type=F32,
            )
            return carry

        lax.fori_loop(first, last, one, 0)

    def give_block(block):
        to_x, to_c = lax.div(block, nc), lax.rem(block, nc)

        @pl.when(block != me)
        def _():
            pltpu.make_async_remote_copy(
                src_ref=proj_z.at[block],
                dst_ref=proj_all.at[me],
                send_sem=px_sems.at[0, block],
                recv_sem=px_sems.at[1, me],
                device_id={"tensor": to_x, "sub": to_c},
                device_id_type=MESH,
            ).start()

        @pl.when(block == me)
        def _():
            proj_all[me] = proj_z[block]

    def proj_step(d):
        ring_step(d, p_part, p_sems)
        pair_send(d, p_part, py_sems) if d > 0 else None
        if d > 1:
            proj_done(d - 1)
        if d == 0:
            give_block(z)

    def proj_done(d):
        pair_wait(d, p_part, py_sems)
        give_block(slab_of(RIGHT, d))
        if d < half:
            give_block(slab_of(LEFT, d))

    ready = min(3, half - 1)
    lag = min(5, half)
    done = 0
    for d in range(1, half + 1):
        ring_step(d, w_part, w_sems)
        pair_send(d, w_part, wy_sems)
        if d > 1:
            pair_wait(d - 1, w_part, wy_sems)
        if d >= lag:
            proj_step(d - lag)
        if d == 1:
            mod_over_seq()
        if d == ready:
            mod_over_plane()
            hide(text_tokens, hidden_text, 1, 0)
            hide(image_tokens, hidden_image, 0, text_rows)
        if d > ready:
            until = min(done + 4, 2 * d - 1)
            project(done, until)
            done = until
    proj_next = half - lag + 1
    pair_wait(half, w_part, wy_sems)
    project(done, nz)

    def normed(values, gain):
        return (
            values
            * lax.rsqrt(jnp.mean(values * values, axis=-1, keepdims=True) + EPSILON)
            * gain
        ).astype(BF16)

    for stream, total, at, count in (
        (1, sum_text, 0, text_rows),
        (0, sum_image, text_rows, image_rows),
    ):
        query[at : at + count, :] = normed(total[:, 0:size], norm_gain[stream, 0])
        key_value[z, at : at + count, 0:size] = normed(
            total[:, size : 2 * size], norm_gain[stream, 1]
        )
        key_value[z, at : at + count, size : 2 * size] = total[:, 2 * size : 3 * size].astype(BF16)

    half_rows = local_rows // 2

    def kv_part(block, part):
        return key_value.at[block, pl.ds(part * half_rows, half_rows), :]

    ring_step(0, kv_part, kv_sems)

    row_max[...] = jnp.full_like(row_max, -1e30)
    row_sum[...] = jnp.zeros_like(row_sum)
    mixed[...] = jnp.zeros_like(mixed)
    factor = float(size) ** (-0.5) * math.log2(math.e)

    def attend(first, last):
        def one(j, carry):
            step = lax.div(j + 1, 2)
            block = wrap(jnp.where(lax.rem(j, 2) == 1, z - step, z + step), nz)
            scores = lax.dot_general(
                query[...],
                key_value[block, :, 0:size],
                (((1,), (1,)), ((), ())),
                preferred_element_type=F32,
            )
            within = lax.broadcasted_iota(jnp.int32, scores.shape, 1)
            usable = (within >= text_rows) | (block * text_rows + within < text_length[0])
            scores = jnp.where(usable, scores, -1e30)
            old = row_max[:, 0:1]
            new = jnp.maximum(old, jnp.max(scores, axis=-1, keepdims=True))
            probs = jnp.exp2((scores - new) * factor)
            fade = jnp.exp2((old - new) * factor)
            row_max[...] = jnp.broadcast_to(new, row_max.shape)
            total = row_sum[:, 0:1] * fade + jnp.sum(probs, axis=-1, keepdims=True)
            row_sum[...] = jnp.broadcast_to(total, row_sum.shape)
            mixed[...] = mixed[...] * fade + jnp.dot(
                probs.astype(BF16),
                key_value[block, :, size : 2 * size],
                preferred_element_type=F32,
            )
            return carry

        lax.fori_loop(first, last, one, 0)

    attend(0, 1)
    for d in range(1, half + 1):
        ring_step(d, kv_part, kv_sems)
        if proj_next <= half:
            proj_step(proj_next)
            proj_next += 1
        attend(2 * d - 1, min(2 * d + 1, nz))
    while proj_next <= half:
        proj_step(proj_next)
        proj_next += 1

    attended[me] = (mixed[...] / row_sum[:, 0:1]).astype(BF16)
    proj_done(half)

    x_half = nx // 2
    x_right, x_left = {"tensor": wrap(x + 1, nx)}, {"tensor": wrap(x - 1, nx)}

    def x_parts(way, d):
        if d < x_half:
            return (0, 1)
        return (0,) if way == RIGHT else (1,)

    def x_block(way, d):
        return (wrap(x - d, nx) if way == RIGHT else wrap(x + d, nx)) * nc + c

    def a_part(block, part):
        return attended.at[block, pl.ds(part * half_rows, half_rows), :]

    for part in (0, 1):
        for way, to in ((RIGHT, x_right), (LEFT, x_left)):
            if part in x_parts(way, 1):
                send(a_part(me, part), a_part(me, part), ax_sems, (way, 1, part), to)
        send(a_part(me, part), a_part(me, part), as_sems, (RIGHT, 0, part), sibling)
    for d in range(1, x_half + 1):
        for part in (0, 1):
            for way, to in ((RIGHT, x_right), (LEFT, x_left)):
                if part not in x_parts(way, d):
                    continue
                block = x_block(way, d)
                arrive(a_part(block, part), ax_sems, (way, d, part), to)
                if d < x_half and part in x_parts(way, d + 1):
                    send(a_part(block, part), a_part(block, part), ax_sems, (way, d + 1, part), to)
                send(a_part(block, part), a_part(block, part), as_sems, (way, d, part), sibling)

    for i in range(1, heads):
        source = wrap(me + i, heads)
        pltpu.make_async_remote_copy(
            src_ref=proj_all.at[source],
            dst_ref=proj_all.at[source],
            send_sem=px_sems.at[0, source],
            recv_sem=px_sems.at[1, source],
            device_id=sibling,
            device_id_type=MESH,
        ).wait_recv()

    across = 1 - 2 * c
    for d in range(0, x_half + 1):
        for part in (0, 1):
            for way in (RIGHT, LEFT):
                if d == 0 and way == LEFT:
                    continue
                if d > 0 and part not in x_parts(way, d):
                    continue
                block = (me if d == 0 else x_block(way, d)) + across
                arrive(a_part(block, part), as_sems, (way, d, part), sibling)

    out_width = image_out.shape[1]
    sum_out = None
    image_sum, text_sum = None, None
    for h in range(0, heads, 2):
        rows = jnp.concatenate([attended[h], attended[h + 1]], axis=1)
        image_w = jnp.concatenate([proj_all[h, 0], proj_all[h + 1, 0]], axis=0)
        text_w = jnp.concatenate([proj_all[h, 1], proj_all[h + 1, 1]], axis=0)
        image_term = jnp.dot(rows[text_rows:], image_w, preferred_element_type=F32)
        text_term = jnp.dot(rows[:text_rows], text_w, preferred_element_type=F32)
        image_sum = image_term if image_sum is None else image_sum + image_term
        text_sum = text_term if text_sum is None else text_sum + text_term

    def own_columns(wide):
        return jnp.where(c == 0, wide[:, :out_width], wide[:, out_width:])

    window = pl.ds(pl.multiple_of(x * 2 * out_width, 128), 2 * out_width)
    for tokens, total, out, stream in (
        (image_tokens, image_sum, image_out, 0),
        (text_tokens, text_sum, text_out, 1),
    ):
        gate = own_columns(mod_piece((stream * 3 + 2) * pieces + x))
        base = own_columns(tokens[:, window].astype(F32))
        out[...] = (base + gate * total).astype(BF16)

    for copy in started:
        copy.wait_send()
    for i in range(1, heads):
        block = wrap(me + i, heads)
        pltpu.make_async_remote_copy(
            src_ref=proj_z.at[block],
            dst_ref=proj_all.at[me],
            send_sem=px_sems.at[0, block],
            recv_sem=px_sems.at[1, me],
            device_id=sibling,
            device_id_type=MESH,
        ).wait_send()


def solution(mesh):
    nz, nx, nc = mesh.shape["seq"], mesh.shape["tensor"], mesh.shape["sub"]
    paired = mesh.shape["groups"] % 2 == 0
    heads = nx * nc

    def body(
        image_tokens,
        text_tokens,
        timestep,
        text_length,
        time_table,
        mod_weight,
        qkv_image,
        qkv_text,
        norm_gain,
        proj_image,
        proj_text,
    ):
        slab = qkv_image.shape[0]
        embedded = lax.dynamic_slice(
            time_table, (timestep[0], lax.axis_index("seq") * slab), (1, slab)
        ).astype(F32)
        vector_rows = jax.nn.silu(embedded).astype(BF16)
        gains = norm_gain.reshape(2, 2, 1, norm_gain.shape[-1])
        image_rows, width = image_tokens.shape
        text_rows = text_tokens.shape[0]
        local_rows = image_rows + text_rows
        columns = qkv_image.shape[1]
        size = columns // 3
        out_width = width // heads
        half = nz // 2
        vmem = pl.BlockSpec(memory_space=pltpu.VMEM)
        anywhere = pl.BlockSpec(memory_space=pl.ANY)
        dma = pltpu.SemaphoreType.DMA
        return pl.pallas_call(
            functools.partial(kernel, (nz, nx, nc), paired),
            out_shape=(
                jax.ShapeDtypeStruct((image_rows, out_width), BF16),
                jax.ShapeDtypeStruct((text_rows, out_width), BF16),
            ),
            in_specs=[pl.BlockSpec(memory_space=pltpu.SMEM)] + [vmem] * 5 + [anywhere] * 4,
            out_specs=(vmem, vmem),
            scratch_shapes=[
                pltpu.VMEM((nz, 1, mod_weight.shape[1]), F32),
                pltpu.VMEM((heads, 1, mod_weight.shape[1]), F32),
                pltpu.VMEM((local_rows, 128), F32),
                pltpu.VMEM((local_rows, 128), F32),
                pltpu.VMEM((nz, image_rows, slab), BF16),
                pltpu.VMEM((nz, text_rows, slab), BF16),
                pltpu.VMEM((nz, slab, 2 * columns), BF16),
                pltpu.VMEM((image_rows, columns), F32),
                pltpu.VMEM((text_rows, columns), F32),
                pltpu.VMEM((nz, 2, *proj_image.shape), BF16),
                pltpu.VMEM((heads, 2, *proj_image.shape), BF16),
                pltpu.VMEM((local_rows, size), BF16),
                pltpu.VMEM((nz, local_rows, 2 * size), BF16),
                pltpu.VMEM((local_rows, 128), F32),
                pltpu.VMEM((local_rows, 128), F32),
                pltpu.VMEM((local_rows, size), F32),
                pltpu.VMEM((heads, local_rows, size), BF16),
                dma((4,)),
                dma((2, nz)),
                dma((2, heads)),
                dma((2, 2, half + 1, 2)),
                dma((2, 2, half + 1)),
                dma((2, 2, half + 1, 2)),
                dma((2, 2, half + 1)),
                dma((2, heads)),
                dma((2, 2, half + 1, 2)),
                dma((2, 2, nx // 2 + 1, 2)),
                dma((2, 2, nx // 2 + 1, 2)),
            ],
            compiler_params=pltpu.CompilerParams(
                collective_id=0, has_side_effects=True, vmem_limit_bytes=56 * 1024 * 1024
            ),
        )(
            text_length,
            vector_rows,
            image_tokens,
            text_tokens,
            mod_weight,
            gains,
            qkv_image,
            qkv_text,
            proj_image,
            proj_text,
        )

    return jax.shard_map(
        body,
        mesh=mesh,
        in_specs=(
            P(("groups", "seq"), None),
            P(("groups", "seq"), None),
            P("groups"),
            P("groups"),
            P(),
            P("seq", ("tensor", "sub")),
            P("seq", ("tensor", "sub")),
            P("seq", ("tensor", "sub")),
            P(None, None, ("tensor", "sub"), None),
            P(("tensor", "sub"), "seq"),
            P(("tensor", "sub"), "seq"),
        ),
        out_specs=(
            P(("groups", "seq"), ("tensor", "sub")),
            P(("groups", "seq"), ("tensor", "sub")),
        ),
        check_vma=False,
    )
```

time: 333 us -> 189 us (0.57)
  the two profiles are of different devices: /device:TPU:65 before, /device:TPU:67 now
where the time goes in v1:
time: 189 us
  Pallas kernels  179 us (95%)
  local copies, waits for them, and re-layouts  6.04 us (3%)
  between operations  1.94 us (1%)
    pallas_call x1, Pallas kernels, body(): pl.pallas_call(functools.partial(kernel, (nz, nx, nc), paired), out_shape...  179 us
    unnamed x3, local copies, waits for them, and re-layouts  4.39 us

profile of v1, /device:TPU:67, one launch (start us, length us, event | category | flops | bytes accessed | tf_op | source)
XLA Modules:
  0.0 188.8 jit_solution(8128330225720830675)
XLA Ops:
  1.9 1.4 fusion.vector_rows
  3.3 1.5 copy.13.proj_image
  4.8 1.5 copy.14.proj_text
  6.3 179.4 %shard_map.122 = (bf16[256,192]{1,0:T(8,128)(2,1)}, bf16[32,192]{1,0:T(8,128)(2,1)}) custom-call(s32[1]{0:T(128)S(6)} %copy.18.text_length, bf16[1,192]{1,0:T(2,128)(2,1)} %fusion.vector_rows, bf16[256,3072]{1,0:T(8,128)(2,1)} %image_tokens.1, bf16[32,3072]{1,0:T(8,128)(2,1)} %text_tokens.1, bf16[192,1152]{1,0:T(8,128)(2,1)} %mod_weight.1, ...), custom_call_target="tpu_custom_call" | custom-call | tf_op jit(solution)/shard_map/pallas_call | solution.py:529
  185.8 1.6 copy.15
  187.4 1.3 copy.19

commit v2 on v1

--- a/solution.py
+++ b/solution.py
@@ -21,27 +21,32 @@
     return pl.ds(pl.multiple_of(start, unit), size)
 
 
-def cut_three(rows, unit, own):
-    third = -(-rows // (3 * unit)) * unit
-    rest = rows - 2 * third
-    return (own * third, third), (2 * third, rest), ((1 - own) * third, third)
+def cut_three(rows, own):
+    alone = -(-rows * 5 // (12 * 16)) * 16
+    return (own * alone, alone), (2 * alone, rows - 2 * alone), ((1 - own) * alone, alone)
 
 
 def kernel(
     sizes,
     paired,
     text_length,
-    vector_rows,
-    image_tokens,
-    text_tokens,
-    mod_weight,
-    norm_gain,
+    timestep,
+    image_hbm,
+    text_hbm,
+    table_hbm,
+    mod_hbm,
+    gain_hbm,
     qkv_image,
     qkv_text,
     proj_image,
     proj_text,
     image_out,
     text_out,
+    image_tokens,
+    text_tokens,
+    time_table,
+    mod_weight,
+    norm_gain,
     mod_z,
     mod_all,
     mean_of,
@@ -49,8 +54,10 @@
     hidden_image,
     hidden_text,
     weights,
+    text_weights,
     sum_image,
     sum_text,
+    text_qkv,
     proj_z,
     proj_all,
     query,
@@ -64,6 +71,9 @@
     modx_sems,
     w_sems,
     wy_sems,
+    t_sems,
+    th_sems,
+    tq_sems,
     p_sems,
     py_sems,
     px_sems,
@@ -86,11 +96,19 @@
     columns = qkv_image.shape[1]
     size = columns // 3
     started = []
+    active = c == own
+
+    def when_active(run):
+        if paired:
+            pl.when(active)(run)
+        else:
+            run()
+
 
     def wrap(i, n):
         return lax.rem(i + n, n)
 
-    def send(src, dst, sems, index, device):
+    def send(src, dst, sems, index, device, keep=True):
         copy = pltpu.make_async_remote_copy(
             src_ref=src,
             dst_ref=dst,
@@ -100,7 +118,8 @@
             device_id_type=MESH,
         )
         copy.start()
-        started.append(copy)
+        if keep:
+            started.append(copy)
 
     def arrive(ref, sems, index, device):
         pltpu.make_async_remote_copy(
@@ -116,15 +135,6 @@
     partner = {"groups": other_group}
     sibling = {"sub": 1 - c}
 
-    loads = [
-        pltpu.make_async_copy(qkv_image, weights.at[z, :, pl.ds(0, columns)], load_sem.at[0]),
-        pltpu.make_async_copy(qkv_text, weights.at[z, :, pl.ds(columns, columns)], load_sem.at[1]),
-        pltpu.make_async_copy(proj_image, proj_z.at[z, 0], load_sem.at[2]),
-        pltpu.make_async_copy(proj_text, proj_z.at[z, 1], load_sem.at[3]),
-    ]
-    for copy in loads:
-        copy.start()
-
     barrier = pltpu.get_barrier_semaphore()
     peers = [{"seq": wrap(z + i, nz)} for i in range(1, nz)]
     plane = [
@@ -135,7 +145,36 @@
     for device in greeted:
         pl.semaphore_signal(barrier, inc=1, device_id=device, device_id_type=MESH)
 
-    mod_z[z] = jnp.dot(vector_rows[...], mod_weight[...], preferred_element_type=F32)
+    piece = 2 * slab
+    table_window = pl.ds(pl.multiple_of(lax.div(z, 2) * piece, 128), piece)
+    loads = [
+        pltpu.make_async_copy(src, dst, load_sem.at[i])
+        for i, (src, dst) in enumerate(
+            (
+                (table_hbm.at[:, table_window], time_table),
+                (mod_hbm, mod_weight),
+                (qkv_image, weights.at[z]),
+                (qkv_text, text_weights.at[z]),
+                (proj_image, proj_z.at[z, 0]),
+                (proj_text, proj_z.at[z, 1]),
+                (text_hbm, text_tokens),
+                (image_hbm, image_tokens),
+                (gain_hbm, norm_gain),
+            )
+        )
+    ]
+    for copy in loads:
+        copy.start()
+    for copy in loads[:6]:
+        copy.wait()
+
+    picked = lax.broadcasted_iota(jnp.int32, time_table.shape, 0) == timestep[0]
+    embedded = jnp.sum(
+        jnp.where(picked, time_table[...].astype(F32), 0.0), axis=0, keepdims=True
+    )
+    vector = (embedded / (1.0 + jnp.exp(-embedded))).astype(BF16)
+    vector_rows = jnp.where(lax.rem(z, 2) == 0, vector[:, :slab], vector[:, slab:])
+    mod_z[z] = jnp.dot(vector_rows, mod_weight[...], preferred_element_type=F32)
 
     chunk = 16
 
@@ -152,12 +191,10 @@
 
         lax.fori_loop(0, tokens.shape[0] // chunk, one, 0)
 
-    for copy in loads:
-        copy.wait()
     pl.semaphore_wait(barrier, len(greeted))
 
     for i in range(1, nz):
-        send(mod_z.at[z], mod_z.at[z], modz_sems, (z,) if False else (i,), {"seq": wrap(z + i, nz)})
+        send(mod_z.at[z], mod_z.at[z], modz_sems, (i,), peers[i - 1])
 
     half = nz // 2
 
@@ -169,14 +206,15 @@
             return (0, 1)
         return (0,) if way == RIGHT else (1,)
 
-    def ring_step(d, part_ref, sems):
+    def ring_step(d, part_ref, sems, keep=True):
         for way, to in ((RIGHT, right), (LEFT, left)):
             block = slab_of(way, d)
             for part in parts_at(way, d):
                 if d > 0:
                     arrive(part_ref(block, part), sems, (way, d, part), to)
                 if d < half and part in parts_at(way, d + 1):
-                    send(part_ref(block, part), part_ref(block, part), sems, (way, d + 1, part), to)
+                    here = part_ref(block, part)
+                    send(here, here, sems, (way, d + 1, part), to, keep)
 
     def pair_send(d, part_ref, sems):
         if not paired:
@@ -194,24 +232,32 @@
                 arrive(part_ref(slab_of(way, d), 2), sems, (way, d), partner)
 
     if paired:
-        w_parts = cut_three(slab, 16, own)
-        p_parts = cut_three(size, 16, own)
+        w_parts = cut_three(slab, own)
     else:
         w_parts = ((0, slab // 2), (slab // 2, slab // 2))
-        p_parts = ((0, size // 2), (size // 2, size // 2))
 
     def w_part(block, part):
         start, count = w_parts[part]
         return weights.at[block, rows_at(start, count), :]
 
+    def t_part(block, part):
+        return text_weights.at[block, pl.ds(part * (slab // 2), slab // 2), :]
+
     def p_part(block, part):
-        start, count = p_parts[part]
+        start, count = w_parts[part]
         return proj_z.at[block, :, rows_at(start, count), :]
 
+    def text_step(d):
+        when_active(lambda: ring_step(d, t_part, t_sems, False))
+
     ring_step(0, w_part, w_sems)
-
-    statistics(text_tokens, 0)
-    statistics(image_tokens, text_rows)
+    text_step(0)
+    ring_step(0, p_part, p_sems)
+
+    for copy in loads[6:]:
+        copy.wait()
+    statistics(text_tokens, image_rows)
+    statistics(image_tokens, 0)
 
     def mod_over_seq():
         for i in range(1, nz):
@@ -229,7 +275,6 @@
             source = wrap(me - i, heads)
             arrive(mod_all.at[source], modx_sems, (i,), plane[i - 1])
 
-    piece = 2 * slab
     per_block = mod_weight.shape[1] // piece
     pieces = width // piece
 
@@ -258,18 +303,14 @@
     sum_image[...] = jnp.zeros_like(sum_image)
     sum_text[...] = jnp.zeros_like(sum_text)
 
-    def project(first, last):
+    def block_at(j):
+        step = lax.div(j + 1, 2)
+        return wrap(jnp.where(lax.rem(j, 2) == 1, z - step, z + step), nz)
+
+    def project(hidden, total, shards, first, last):
         def one(j, carry):
-            step = lax.div(j + 1, 2)
-            block = wrap(jnp.where(lax.rem(j, 2) == 1, z - step, z + step), nz)
-            sum_image[...] += jnp.dot(
-                hidden_image[block], weights[block, :, 0:columns], preferred_element_type=F32
-            )
-            sum_text[...] += jnp.dot(
-                hidden_text[block],
-                weights[block, :, columns : 2 * columns],
-                preferred_element_type=F32,
-            )
+            block = block_at(j)
+            total[...] += jnp.dot(hidden[block], shards[block], preferred_element_type=F32)
             return carry
 
         lax.fori_loop(first, last, one, 0)
@@ -292,43 +333,43 @@
         def _():
             proj_all[me] = proj_z[block]
 
-    def proj_step(d):
-        ring_step(d, p_part, p_sems)
-        pair_send(d, p_part, py_sems) if d > 0 else None
-        if d > 1:
-            proj_done(d - 1)
-        if d == 0:
-            give_block(z)
-
     def proj_done(d):
         pair_wait(d, p_part, py_sems)
         give_block(slab_of(RIGHT, d))
-        if d < half:
+        if 0 < d < half:
             give_block(slab_of(LEFT, d))
 
+    give_block(z)
     ready = min(3, half - 1)
-    lag = min(5, half)
     done = 0
+    both = hidden_text.at[:, pl.ds(0, text_rows), :], hidden_text.at[:, pl.ds(text_rows, text_rows), :]
     for d in range(1, half + 1):
         ring_step(d, w_part, w_sems)
+        text_step(d)
         pair_send(d, w_part, wy_sems)
-        if d > 1:
-            pair_wait(d - 1, w_part, wy_sems)
-        if d >= lag:
-            proj_step(d - lag)
+        ring_step(d, p_part, p_sems)
+        pair_send(d, p_part, py_sems)
         if d == 1:
             mod_over_seq()
         if d == ready:
             mod_over_plane()
-            hide(text_tokens, hidden_text, 1, 0)
-            hide(image_tokens, hidden_image, 0, text_rows)
+            hide(text_tokens, hidden_text, 1, image_rows)
+            if paired:
+
+                @pl.when(jnp.logical_not(active))
+                def _():
+                    send(both[0], both[1], th_sems, (), partner, False)
+
+            hide(image_tokens, hidden_image, 0, 0)
+        if d > 1:
+            pair_wait(d - 1, w_part, wy_sems)
+            proj_done(d - 1)
         if d > ready:
             until = min(done + 4, 2 * d - 1)
-            project(done, until)
+            project(hidden_image, sum_image, weights, done, until)
             done = until
-    proj_next = half - lag + 1
     pair_wait(half, w_part, wy_sems)
-    project(done, nz)
+    project(hidden_image, sum_image, weights, done, nz)
 
     def normed(values, gain):
         return (
@@ -337,22 +378,51 @@
             * gain
         ).astype(BF16)
 
-    for stream, total, at, count in (
-        (1, sum_text, 0, text_rows),
-        (0, sum_image, text_rows, image_rows),
-    ):
-        query[at : at + count, :] = normed(total[:, 0:size], norm_gain[stream, 0])
-        key_value[z, at : at + count, 0:size] = normed(
-            total[:, size : 2 * size], norm_gain[stream, 1]
+    def normed_three(total, stream):
+        return (
+            normed(total[:, 0:size], norm_gain[stream, 0]),
+            normed(total[:, size : 2 * size], norm_gain[stream, 1]),
+            total[:, 2 * size : 3 * size].astype(BF16),
         )
-        key_value[z, at : at + count, size : 2 * size] = total[:, 2 * size : 3 * size].astype(BF16)
 
     half_rows = local_rows // 2
 
     def kv_part(block, part):
         return key_value.at[block, pl.ds(part * half_rows, half_rows), :]
 
-    ring_step(0, kv_part, kv_sems)
+    def kv_send(part):
+        for way, to in ((RIGHT, right), (LEFT, left)):
+            if part in parts_at(way, 1):
+                send(kv_part(z, part), kv_part(z, part), kv_sems, (way, 1, part), to)
+
+    q, k, v = normed_three(sum_image[...], 0)
+    query[0:image_rows, :] = q
+    key_value[z, 0:image_rows, 0:size] = k
+    key_value[z, 0:image_rows, size : 2 * size] = v
+    kv_send(0)
+
+    def text_projection():
+        if paired:
+            arrive(both[1], th_sems, (), partner)
+        project(hidden_text, sum_text, text_weights, 0, nz)
+        for side in (0, 1) if paired else (0,):
+            parts = normed_three(sum_text[side * text_rows : (side + 1) * text_rows, :], 1)
+            for i in range(3):
+                text_qkv[side, :, i * size : (i + 1) * size] = parts[i]
+        if paired:
+            send(text_qkv.at[1], text_qkv.at[0], tq_sems, (), partner, False)
+
+    when_active(text_projection)
+    if paired:
+
+        @pl.when(jnp.logical_not(active))
+        def _():
+            arrive(text_qkv.at[0], tq_sems, (), partner)
+
+    query[image_rows:, :] = text_qkv[0, :, 0:size]
+    key_value[z, image_rows:, :] = text_qkv[0, :, size : 3 * size]
+    kv_send(1)
+    proj_done(half)
 
     row_max[...] = jnp.full_like(row_max, -1e30)
     row_sum[...] = jnp.zeros_like(row_sum)
@@ -361,8 +431,7 @@
 
     def attend(first, last):
         def one(j, carry):
-            step = lax.div(j + 1, 2)
-            block = wrap(jnp.where(lax.rem(j, 2) == 1, z - step, z + step), nz)
+            block = block_at(j)
             scores = lax.dot_general(
                 query[...],
                 key_value[block, :, 0:size],
@@ -370,7 +439,8 @@
                 preferred_element_type=F32,
             )
             within = lax.broadcasted_iota(jnp.int32, scores.shape, 1)
-            usable = (within >= text_rows) | (block * text_rows + within < text_length[0])
+            slot = block * text_rows + within - image_rows
+            usable = (within < image_rows) | (slot < text_length[0])
             scores = jnp.where(usable, scores, -1e30)
             old = row_max[:, 0:1]
             new = jnp.maximum(old, jnp.max(scores, axis=-1, keepdims=True))
@@ -391,16 +461,9 @@
     attend(0, 1)
     for d in range(1, half + 1):
         ring_step(d, kv_part, kv_sems)
-        if proj_next <= half:
-            proj_step(proj_next)
-            proj_next += 1
         attend(2 * d - 1, min(2 * d + 1, nz))
-    while proj_next <= half:
-        proj_step(proj_next)
-        proj_next += 1
 
     attended[me] = (mixed[...] / row_sum[:, 0:1]).astype(BF16)
-    proj_done(half)
 
     x_half = nx // 2
     x_right, x_left = {"tensor": wrap(x + 1, nx)}, {"tensor": wrap(x - 1, nx)}
@@ -455,14 +518,16 @@
                 arrive(a_part(block, part), as_sems, (way, d, part), sibling)
 
     out_width = image_out.shape[1]
-    sum_out = None
     image_sum, text_sum = None, None
     for h in range(0, heads, 2):
         rows = jnp.concatenate([attended[h], attended[h + 1]], axis=1)
-        image_w = jnp.concatenate([proj_all[h, 0], proj_all[h + 1, 0]], axis=0)
-        text_w = jnp.concatenate([proj_all[h, 1], proj_all[h + 1, 1]], axis=0)
-        image_term = jnp.dot(rows[text_rows:], image_w, preferred_element_type=F32)
-        text_term = jnp.dot(rows[:text_rows], text_w, preferred_element_type=F32)
+        image_w = jnp.concatenate([proj_all[h, 0], proj_all[h + 1, 0]], axis=1)
+        text_w = jnp.concatenate([proj_all[h, 1], proj_all[h + 1, 1]], axis=1)
+        turned = (((1,), (1,)), ((), ()))
+        image_term = lax.dot_general(
+            rows[:image_rows], image_w, turned, preferred_element_type=F32
+        )
+        text_term = lax.dot_general(rows[image_rows:], text_w, turned, preferred_element_type=F32)
         image_sum = image_term if image_sum is None else image_sum + image_term
         text_sum = text_term if text_sum is None else text_sum + text_term
 
@@ -480,6 +545,32 @@
 
     for copy in started:
         copy.wait_send()
+
+    def sent(ref, sems, index, device):
+        pltpu.make_async_remote_copy(
+            src_ref=ref,
+            dst_ref=ref,
+            send_sem=sems.at[(0, *index)],
+            recv_sem=sems.at[(1, *index)],
+            device_id=device,
+            device_id_type=MESH,
+        ).wait_send()
+
+    def text_sent():
+        for d in range(1, half + 1):
+            for way, to in ((RIGHT, right), (LEFT, left)):
+                for part in parts_at(way, d):
+                    sent(t_part(z, part), t_sems, (way, d, part), to)
+        if paired:
+            sent(text_qkv.at[1], tq_sems, (), partner)
+
+    when_active(text_sent)
+    if paired:
+
+        @pl.when(jnp.logical_not(active))
+        def _():
+            sent(both[0], th_sems, (), partner)
+
     for i in range(1, heads):
         block = wrap(me + i, heads)
         pltpu.make_async_remote_copy(
@@ -511,10 +602,6 @@
         proj_text,
     ):
         slab = qkv_image.shape[0]
-        embedded = lax.dynamic_slice(
-            time_table, (timestep[0], lax.axis_index("seq") * slab), (1, slab)
-        ).astype(F32)
-        vector_rows = jax.nn.silu(embedded).astype(BF16)
         gains = norm_gain.reshape(2, 2, 1, norm_gain.shape[-1])
         image_rows, width = image_tokens.shape
         text_rows = text_tokens.shape[0]
@@ -532,31 +619,41 @@
                 jax.ShapeDtypeStruct((image_rows, out_width), BF16),
                 jax.ShapeDtypeStruct((text_rows, out_width), BF16),
             ),
-            in_specs=[pl.BlockSpec(memory_space=pltpu.SMEM)] + [vmem] * 5 + [anywhere] * 4,
+            in_specs=[pl.BlockSpec(memory_space=pltpu.SMEM)] * 2 + [anywhere] * 9,
             out_specs=(vmem, vmem),
             scratch_shapes=[
+                pltpu.VMEM(image_tokens.shape, BF16),
+                pltpu.VMEM(text_tokens.shape, BF16),
+                pltpu.VMEM((time_table.shape[0], 2 * slab), BF16),
+                pltpu.VMEM(mod_weight.shape, BF16),
+                pltpu.VMEM(gains.shape, F32),
                 pltpu.VMEM((nz, 1, mod_weight.shape[1]), F32),
                 pltpu.VMEM((heads, 1, mod_weight.shape[1]), F32),
                 pltpu.VMEM((local_rows, 128), F32),
                 pltpu.VMEM((local_rows, 128), F32),
                 pltpu.VMEM((nz, image_rows, slab), BF16),
-                pltpu.VMEM((nz, text_rows, slab), BF16),
-                pltpu.VMEM((nz, slab, 2 * columns), BF16),
+                pltpu.VMEM((nz, 2 * text_rows, slab), BF16),
+                pltpu.VMEM((nz, slab, columns), BF16),
+                pltpu.VMEM((nz, slab, columns), BF16),
                 pltpu.VMEM((image_rows, columns), F32),
-                pltpu.VMEM((text_rows, columns), F32),
-                pltpu.VMEM((nz, 2, *proj_image.shape), BF16),
-                pltpu.VMEM((heads, 2, *proj_image.shape), BF16),
+                pltpu.VMEM((2 * text_rows, columns), F32),
+                pltpu.VMEM((2, text_rows, columns), BF16),
+                pltpu.VMEM((nz, 2, *proj_image.shape[::-1]), BF16),
+                pltpu.VMEM((heads, 2, *proj_image.shape[::-1]), BF16),
                 pltpu.VMEM((local_rows, size), BF16),
                 pltpu.VMEM((nz, local_rows, 2 * size), BF16),
                 pltpu.VMEM((local_rows, 128), F32),
                 pltpu.VMEM((local_rows, 128), F32),
                 pltpu.VMEM((local_rows, size), F32),
                 pltpu.VMEM((heads, local_rows, size), BF16),
-                dma((4,)),
+                dma((9,)),
                 dma((2, nz)),
                 dma((2, heads)),
                 dma((2, 2, half + 1, 2)),
                 dma((2, 2, half + 1)),
+                dma((2, 2, half + 1, 2)),
+                dma((2,)),
+                dma((2,)),
                 dma((2, 2, half + 1, 2)),
                 dma((2, 2, half + 1)),
                 dma((2, heads)),
@@ -569,15 +666,16 @@
             ),
         )(
             text_length,
-            vector_rows,
+            timestep,
             image_tokens,
             text_tokens,
+            time_table,
             mod_weight,
             gains,
             qkv_image,
             qkv_text,
-            proj_image,
-            proj_text,
+            proj_image.T,
+            proj_text.T,
         )
 
     return jax.shard_map(

time: 189 us -> 160 us (0.85)
  the two profiles are of different devices: /device:TPU:67 before, /device:TPU:65 now
where the time goes in v2:
time: 160 us; the launch traced here: 159 us
  Pallas kernels  154 us (96%)
  local copies, waits for them, and re-layouts  2.97 us (2%)
  between operations  1.93 us (1%)
    pallas_call x1, Pallas kernels, body(): pl.pallas_call(functools.partial(kernel, (nz, nx, nc), paired), out_shape...  154 us

profile of v2, /device:TPU:65, one launch (start us, length us, event | category | flops | bytes accessed | tf_op | source)
XLA Modules:
  0.0 159.0 jit_solution(17951256968035771587)
XLA Ops:
  1.9 154.1 %shard_map.122 = (bf16[256,192]{1,0:T(8,128)(2,1)}, bf16[32,192]{1,0:T(8,128)(2,1)}) custom-call(s32[1]{0:T(128)S(6)} %copy.16.text_length, s32[1]{0:T(128)S(6)} %copy.15.timestep, bf16[256,3072]{1,0:T(8,128)(2,1)} %image_hbm.1, bf16[32,3072]{1,0:T(8,128)(2,1)} %text_hbm.1, bf16[50,3072]{1,0:T(8,128)(2,1)} %table_hbm.1, bf16[192,1152]{1,0:T(8,128)(2,1)} %mod_hbm.1, ...), custom_call_target="tpu_custom_call" | custom-call | tf_op jit(solution)/shard_map/pallas_call | solution.py:616
  156.1 1.6 %copy.13 = bf16[256,192]{0,1:T(8,128)(2,1)} copy(bf16[256,192]{1,0:T(8,128)(2,1)} %get-tuple-element.2) | data formatting | bytes 196608 | tf_op jit(solution)/shard_map/pallas_call | solution.py:616
  157.7 1.3 copy.17

commit v3 on v2

--- a/solution.py
+++ b/solution.py
@@ -19,11 +19,6 @@
     if isinstance(start, int):
         return pl.ds(start, size)
     return pl.ds(pl.multiple_of(start, unit), size)
-
-
-def cut_three(rows, own):
-    alone = -(-rows * 5 // (12 * 16)) * 16
-    return (own * alone, alone), (2 * alone, rows - 2 * alone), ((1 - own) * alone, alone)
 
 
 def kernel(
@@ -67,21 +62,24 @@
     mixed,
     attended,
     load_sem,
-    modz_sems,
-    modx_sems,
-    w_sems,
-    wy_sems,
-    t_sems,
-    th_sems,
-    tq_sems,
-    p_sems,
-    py_sems,
-    px_sems,
-    kv_sems,
-    ax_sems,
-    as_sems,
+    *pairs,
 ):
     nz, nx, nc = sizes
+    (
+        modz_sems,
+        modx_sems,
+        w_sems,
+        wy_sems,
+        t_sems,
+        th_sems,
+        tq_sems,
+        p_sems,
+        py_sems,
+        px_sems,
+        kv_sems,
+        ax_sems,
+        as_sems,
+    ) = zip(pairs[0::2], pairs[1::2])
     heads = nx * nc
     z = lax.axis_index("seq")
     x = lax.axis_index("tensor")
@@ -95,7 +93,6 @@
     slab = qkv_image.shape[0]
     columns = qkv_image.shape[1]
     size = columns // 3
-    started = []
     active = c == own
 
     def when_active(run):
@@ -108,28 +105,24 @@
     def wrap(i, n):
         return lax.rem(i + n, n)
 
-    def send(src, dst, sems, index, device, keep=True):
-        copy = pltpu.make_async_remote_copy(
+    def copy_of(src, dst, sems, index, device):
+        return pltpu.make_async_remote_copy(
             src_ref=src,
             dst_ref=dst,
-            send_sem=sems.at[(0, *index)],
-            recv_sem=sems.at[(1, *index)],
+            send_sem=sems[0].at[0],
+            recv_sem=sems[1].at[index],
             device_id=device,
             device_id_type=MESH,
         )
-        copy.start()
-        if keep:
-            started.append(copy)
+
+    def send(src, dst, sems, index, device):
+        copy_of(src, dst, sems, index, device).start()
 
     def arrive(ref, sems, index, device):
-        pltpu.make_async_remote_copy(
-            src_ref=ref,
-            dst_ref=ref,
-            send_sem=sems.at[(0, *index)],
-            recv_sem=sems.at[(1, *index)],
-            device_id=device,
-            device_id_type=MESH,
-        ).wait_recv()
+        copy_of(ref, ref, sems, index, device).wait_recv()
+
+    def sent(ref, sems, index, device):
+        copy_of(ref, ref, sems, index, device).wait_send()
 
     right, left = {"seq": wrap(z + 1, nz)}, {"seq": wrap(z - 1, nz)}
     partner = {"groups": other_group}
@@ -178,7 +171,7 @@
 
     chunk = 16
 
-    def statistics(tokens, at):
+    def statistics(tokens, first, last, at):
         def one(i, carry):
             rows = rows_at(i * chunk, chunk)
             values = tokens[rows, :].astype(F32)
@@ -189,91 +182,87 @@
             rstd_of[out, :] = jnp.broadcast_to(lax.rsqrt(spread + EPSILON), (chunk, 128))
             return carry
 
-        lax.fori_loop(0, tokens.shape[0] // chunk, one, 0)
+        lax.fori_loop(first // chunk, last // chunk, one, 0)
 
     pl.semaphore_wait(barrier, len(greeted))
 
     for i in range(1, nz):
-        send(mod_z.at[z], mod_z.at[z], modz_sems, (i,), peers[i - 1])
+        send(mod_z.at[z], mod_z.at[z], modz_sems, (0,), peers[i - 1])
 
     half = nz // 2
 
     def slab_of(way, d):
         return wrap(z - d, nz) if way == RIGHT else wrap(z + d, nz)
 
-    def parts_at(way, d):
-        if d < half:
-            return (0, 1)
-        return (0,) if way == RIGHT else (1,)
-
-    def ring_step(d, part_ref, sems, keep=True):
+    def carried(way, d, part, parts):
+        return d < half or (part < parts // 2) == (way == RIGHT)
+
+    def ring_part(d, part, parts, part_ref, sems):
         for way, to in ((RIGHT, right), (LEFT, left)):
-            block = slab_of(way, d)
-            for part in parts_at(way, d):
-                if d > 0:
-                    arrive(part_ref(block, part), sems, (way, d, part), to)
-                if d < half and part in parts_at(way, d + 1):
-                    here = part_ref(block, part)
-                    send(here, here, sems, (way, d + 1, part), to, keep)
-
-    def pair_send(d, part_ref, sems):
-        if not paired:
-            return
-        for way in (RIGHT, LEFT):
-            if 0 in parts_at(way, d):
-                block = slab_of(way, d)
-                send(part_ref(block, 0), part_ref(block, 0), sems, (way, d), partner)
-
-    def pair_wait(d, part_ref, sems):
-        if not paired:
-            return
-        for way in (RIGHT, LEFT):
-            if 0 in parts_at(way, d):
-                arrive(part_ref(slab_of(way, d), 2), sems, (way, d), partner)
-
-    if paired:
-        w_parts = cut_three(slab, own)
-    else:
-        w_parts = ((0, slab // 2), (slab // 2, slab // 2))
+            if not carried(way, d, part, parts):
+                continue
+            here = part_ref(slab_of(way, d), part)
+            if d > 0:
+                arrive(here, sems, (way, d - 1, part), to)
+            if d < half and carried(way, d + 1, part, parts):
+                send(here, here, sems, (way, d, part), to)
+
+    share = slab // 2 if paired else slab
 
     def w_part(block, part):
-        start, count = w_parts[part]
-        return weights.at[block, rows_at(start, count), :]
+        return weights.at[block, rows_at(own * share + part * (share // 2), share // 2), :]
+
+    def w_share(block, of):
+        return weights.at[block, rows_at(of * share, share), :]
 
     def t_part(block, part):
         return text_weights.at[block, pl.ds(part * (slab // 2), slab // 2), :]
 
     def p_part(block, part):
-        start, count = w_parts[part]
-        return proj_z.at[block, :, rows_at(start, count), :]
-
-    def text_step(d):
-        when_active(lambda: ring_step(d, t_part, t_sems, False))
-
-    ring_step(0, w_part, w_sems)
-    text_step(0)
-    ring_step(0, p_part, p_sems)
+        return proj_z.at[block, :, rows_at(own * share + part * (share // 2), share // 2), :]
+
+    def p_share(ref, block):
+        return ref.at[block, :, rows_at(own * share, share), :]
+
+    def weight_step(d, tasks=((), ())):
+        for part in (0, 1):
+            ring_part(d, part, 2, w_part, w_sems)
+            when_active(lambda: ring_part(d, part, 2, t_part, t_sems))
+            if part == 0:
+                for task in tasks[0]:
+                    task()
+        if paired and d > 0:
+            for way in (RIGHT, LEFT):
+                if way == RIGHT or d < half:
+                    here = w_share(slab_of(way, d), own)
+                    send(here, here, wy_sems, (way, d - 1), partner)
+        for task in tasks[1]:
+            task()
+
+    def weight_wait(d):
+        if paired:
+            for way in (RIGHT, LEFT):
+                if way == RIGHT or d < half:
+                    arrive(w_share(slab_of(way, d), 1 - own), wy_sems, (way, d - 1), partner)
+
+    weight_step(0)
 
     for copy in loads[6:]:
         copy.wait()
-    statistics(text_tokens, image_rows)
-    statistics(image_tokens, 0)
+    statistics(text_tokens, 0, text_rows, image_rows)
+    statistics(image_tokens, 0, image_rows // 2, 0)
 
     def mod_over_seq():
-        for i in range(1, nz):
-            source = wrap(z - i, nz)
-            arrive(mod_z.at[source], modz_sems, (i,), {"seq": source})
+        arrive(mod_z.at[pl.ds(0, nz - 1)], modz_sems, (0,), right)
         total = mod_z[0]
         for i in range(1, nz):
             total = total + mod_z[i]
         mod_all[me] = total
-        for i in range(1, heads):
-            send(mod_all.at[me], mod_all.at[me], modx_sems, (i,), plane[i - 1])
+        for device in plane:
+            send(mod_all.at[me], mod_all.at[me], modx_sems, (0,), device)
 
     def mod_over_plane():
-        for i in range(1, heads):
-            source = wrap(me - i, heads)
-            arrive(mod_all.at[source], modx_sems, (i,), plane[i - 1])
+        arrive(mod_all.at[pl.ds(0, heads - 1)], modx_sems, (0,), sibling)
 
     per_block = mod_weight.shape[1] // piece
     pieces = width // piece
@@ -284,7 +273,7 @@
         offset = pl.multiple_of(lax.rem(index, per_block) * piece, 128)
         return mod_all[lax.div(index, per_block), :, pl.ds(offset, piece)]
 
-    def hide(tokens, hidden, stream, at):
+    def hide(tokens, hidden, stream, first, last, at):
         def one(i, carry):
             rows = rows_at(i * chunk, chunk)
             out = rows_at(at + i * chunk, chunk)
@@ -298,7 +287,7 @@
                 hidden[2 * p + 1, rows, :] = values[:, slab:]
             return carry
 
-        lax.fori_loop(0, tokens.shape[0] // chunk, one, 0)
+        lax.fori_loop(first // chunk, last // chunk, one, 0)
 
     sum_image[...] = jnp.zeros_like(sum_image)
     sum_text[...] = jnp.zeros_like(sum_text)
@@ -316,60 +305,117 @@
         lax.fori_loop(first, last, one, 0)
 
     def give_block(block):
-        to_x, to_c = lax.div(block, nc), lax.rem(block, nc)
+        target = {"tensor": lax.div(block, nc), "sub": lax.rem(block, nc)}
 
         @pl.when(block != me)
         def _():
-            pltpu.make_async_remote_copy(
-                src_ref=proj_z.at[block],
-                dst_ref=proj_all.at[me],
-                send_sem=px_sems.at[0, block],
-                recv_sem=px_sems.at[1, me],
-                device_id={"tensor": to_x, "sub": to_c},
-                device_id_type=MESH,
-            ).start()
+            send(p_share(proj_z, block), p_share(proj_all, me), px_sems, (0,), target)
 
         @pl.when(block == me)
         def _():
-            proj_all[me] = proj_z[block]
-
-    def proj_done(d):
-        pair_wait(d, p_part, py_sems)
+            rows = rows_at(own * share, share)
+            proj_all[me, :, rows, :] = proj_z[block, :, rows, :]
+
+    def proj_step(d):
+        for part in (0, 1):
+            ring_part(d, part, 2, p_part, p_sems)
         give_block(slab_of(RIGHT, d))
         if 0 < d < half:
             give_block(slab_of(LEFT, d))
 
-    give_block(z)
-    ready = min(3, half - 1)
+    away = lax.rem(z - me + nz, nz)
+    away = jnp.minimum(away, nz - away)
+    all_shares = proj_all.at[:, :, rows_at(own * share, share), :]
+    other_shares = proj_all.at[:, :, rows_at((1 - own) * share, share), :]
+
+    def hand_over(d):
+        @pl.when(away == d)
+        def _():
+            arrive(proj_all.at[pl.ds(0, heads - 1), :, pl.ds(0, share), :], px_sems, (0,), sibling)
+            if paired:
+                send(all_shares, all_shares, py_sems, (0,), partner)
+
+    lag = min(5, half)
+    proj_plan = {}
+    for d in range(half + 1):
+        proj_plan.setdefault(lag + d, []).append((proj_step, d))
+        after = max(lag + d + 3, half + 1 + (d + 1) // 2)
+        proj_plan.setdefault(min(after, 2 * half + 1), []).append((hand_over, d))
+
+    def proj_advance(step):
+        for call, d in proj_plan.get(step, ()):
+            call(d)
+
+    def hidden_exchange():
+        if paired:
+
+            @pl.when(jnp.logical_not(active))
+            def _():
+                send(both[0], both[1], th_sems, (0,), partner)
+
+    both = (
+        hidden_text.at[:, pl.ds(0, text_rows), :],
+        hidden_text.at[:, pl.ds(text_rows, text_rows), :],
+    )
+    middle = image_rows // 2
+
+    def project_all(first, last):
+        project(hidden_image, sum_image, weights, first, last)
+        when_active(lambda: project(hidden_text, sum_text, text_weights, first, last))
+
+    def receive_hidden():
+        if paired:
+            when_active(lambda: arrive(both[1], th_sems, (0,), partner))
+
+    def stats_of(first):
+        return lambda: statistics(image_tokens, first, first + middle // 2, 0)
+
+    def hide_of(first):
+        return lambda: hide(image_tokens, hidden_image, 0, first, first + middle // 2, 0)
+
+    def hide_text():
+        mod_over_plane()
+        hide(text_tokens, hidden_text, 1, 0, text_rows, image_rows)
+        hidden_exchange()
+
     done = 0
-    both = hidden_text.at[:, pl.ds(0, text_rows), :], hidden_text.at[:, pl.ds(text_rows, text_rows), :]
+
+    def multiply(until):
+        def run():
+            nonlocal done
+            project_all(done, until)
+            done = max(done, until)
+
+        return run
+
+    quarter_rows = middle // 2
+    early = [
+        (1, 0, stats_of(middle)),
+        (1, 1, stats_of(middle + quarter_rows)),
+        (2, 1, mod_over_seq),
+        (4, 0, hide_text),
+        (4, 1, hide_of(0)),
+        (5, 0, hide_of(quarter_rows)),
+        (5, 1, hide_of(middle)),
+        (6, 0, hide_of(middle + quarter_rows)),
+        (6, 0, receive_hidden),
+    ]
+    if half >= 8:
+        early += [(6, 1, multiply(3)), (7, 0, multiply(6)), (7, 1, multiply(9)), (8, 0, multiply(11))]
     for d in range(1, half + 1):
-        ring_step(d, w_part, w_sems)
-        text_step(d)
-        pair_send(d, w_part, wy_sems)
-        ring_step(d, p_part, p_sems)
-        pair_send(d, p_part, py_sems)
-        if d == 1:
-            mod_over_seq()
-        if d == ready:
-            mod_over_plane()
-            hide(text_tokens, hidden_text, 1, image_rows)
-            if paired:
-
-                @pl.when(jnp.logical_not(active))
-                def _():
-                    send(both[0], both[1], th_sems, (), partner, False)
-
-            hide(image_tokens, hidden_image, 0, 0)
-        if d > 1:
-            pair_wait(d - 1, w_part, wy_sems)
-            proj_done(d - 1)
-        if d > ready:
-            until = min(done + 4, 2 * d - 1)
-            project(hidden_image, sum_image, weights, done, until)
-            done = until
-    pair_wait(half, w_part, wy_sems)
-    project(hidden_image, sum_image, weights, done, nz)
+        tasks = [
+            [task for at, place, task in early if (min(at, half), place if at < half else 1) == (d, p)]
+            if d < half or p == 1
+            else []
+            for p in (0, 1)
+        ]
+        weight_step(d, tasks)
+        proj_advance(d)
+        if d > 2:
+            weight_wait(d - 2)
+    for d in range(max(1, half - 1), half + 1):
+        weight_wait(d)
+        multiply(min(2 * d + 1, nz))()
 
     def normed(values, gain):
         return (
@@ -385,44 +431,37 @@
             total[:, 2 * size : 3 * size].astype(BF16),
         )
 
-    half_rows = local_rows // 2
+    quarter = local_rows // 64 * 16
+    starts = (0, local_rows // 2 - quarter, local_rows // 2, local_rows - quarter, local_rows)
 
     def kv_part(block, part):
-        return key_value.at[block, pl.ds(part * half_rows, half_rows), :]
-
-    def kv_send(part):
-        for way, to in ((RIGHT, right), (LEFT, left)):
-            if part in parts_at(way, 1):
-                send(kv_part(z, part), kv_part(z, part), kv_sems, (way, 1, part), to)
+        return key_value.at[block, pl.ds(starts[part], starts[part + 1] - starts[part]), :]
 
     q, k, v = normed_three(sum_image[...], 0)
     query[0:image_rows, :] = q
     key_value[z, 0:image_rows, 0:size] = k
     key_value[z, 0:image_rows, size : 2 * size] = v
-    kv_send(0)
+    for part in (0, 1, 2):
+        ring_part(0, part, 4, kv_part, kv_sems)
 
     def text_projection():
-        if paired:
-            arrive(both[1], th_sems, (), partner)
-        project(hidden_text, sum_text, text_weights, 0, nz)
         for side in (0, 1) if paired else (0,):
             parts = normed_three(sum_text[side * text_rows : (side + 1) * text_rows, :], 1)
             for i in range(3):
                 text_qkv[side, :, i * size : (i + 1) * size] = parts[i]
         if paired:
-            send(text_qkv.at[1], text_qkv.at[0], tq_sems, (), partner, False)
+            send(text_qkv.at[1], text_qkv.at[0], tq_sems, (0,), partner)
 
     when_active(text_projection)
     if paired:
 
         @pl.when(jnp.logical_not(active))
         def _():
-            arrive(text_qkv.at[0], tq_sems, (), partner)
+            arrive(text_qkv.at[0], tq_sems, (0,), partner)
 
     query[image_rows:, :] = text_qkv[0, :, 0:size]
     key_value[z, image_rows:, :] = text_qkv[0, :, size : 3 * size]
-    kv_send(1)
-    proj_done(half)
+    ring_part(0, 3, 4, kv_part, kv_sems)
 
     row_max[...] = jnp.full_like(row_max, -1e30)
     row_sum[...] = jnp.zeros_like(row_sum)
@@ -458,20 +497,26 @@
 
         lax.fori_loop(first, last, one, 0)
 
-    attend(0, 1)
     for d in range(1, half + 1):
-        ring_step(d, kv_part, kv_sems)
-        attend(2 * d - 1, min(2 * d + 1, nz))
+        for part in (0, 1):
+            ring_part(d, part, 4, kv_part, kv_sems)
+        attend(max(2 * d - 3, 0), 2 * d - 2 if d > 1 else 1)
+        for part in (2, 3):
+            ring_part(d, part, 4, kv_part, kv_sems)
+        proj_advance(half + d)
+        if d > 1:
+            attend(2 * d - 2, 2 * d - 1)
+    proj_advance(2 * half + 1)
+    attend(nz - 1, nz)
 
     attended[me] = (mixed[...] / row_sum[:, 0:1]).astype(BF16)
 
     x_half = nx // 2
     x_right, x_left = {"tensor": wrap(x + 1, nx)}, {"tensor": wrap(x - 1, nx)}
-
-    def x_parts(way, d):
-        if d < x_half:
-            return (0, 1)
-        return (0,) if way == RIGHT else (1,)
+    half_rows = local_rows // 2
+
+    def x_carried(way, d, part):
+        return d < x_half or (part == 0) == (way == RIGHT)
 
     def x_block(way, d):
         return (wrap(x - d, nx) if way == RIGHT else wrap(x + d, nx)) * nc + c
@@ -479,43 +524,30 @@
     def a_part(block, part):
         return attended.at[block, pl.ds(part * half_rows, half_rows), :]
 
-    for part in (0, 1):
-        for way, to in ((RIGHT, x_right), (LEFT, x_left)):
-            if part in x_parts(way, 1):
-                send(a_part(me, part), a_part(me, part), ax_sems, (way, 1, part), to)
-        send(a_part(me, part), a_part(me, part), as_sems, (RIGHT, 0, part), sibling)
-    for d in range(1, x_half + 1):
+    for d in range(0, x_half + 1):
         for part in (0, 1):
             for way, to in ((RIGHT, x_right), (LEFT, x_left)):
-                if part not in x_parts(way, d):
+                if not x_carried(way, d, part):
                     continue
-                block = x_block(way, d)
-                arrive(a_part(block, part), ax_sems, (way, d, part), to)
-                if d < x_half and part in x_parts(way, d + 1):
-                    send(a_part(block, part), a_part(block, part), ax_sems, (way, d + 1, part), to)
-                send(a_part(block, part), a_part(block, part), as_sems, (way, d, part), sibling)
-
-    for i in range(1, heads):
-        source = wrap(me + i, heads)
-        pltpu.make_async_remote_copy(
-            src_ref=proj_all.at[source],
-            dst_ref=proj_all.at[source],
-            send_sem=px_sems.at[0, source],
-            recv_sem=px_sems.at[1, source],
-            device_id=sibling,
-            device_id_type=MESH,
-        ).wait_recv()
+                here = a_part(x_block(way, d), part)
+                if d > 0:
+                    arrive(here, ax_sems, (way, d - 1, part), to)
+                if d < x_half and x_carried(way, d + 1, part):
+                    send(here, here, ax_sems, (way, d, part), to)
+                if d > 0 or way == RIGHT:
+                    send(here, here, as_sems, (way, d, part), sibling)
+
+    if paired:
+        arrive(other_shares, py_sems, (0,), partner)
 
     across = 1 - 2 * c
     for d in range(0, x_half + 1):
         for part in (0, 1):
             for way in (RIGHT, LEFT):
-                if d == 0 and way == LEFT:
-                    continue
-                if d > 0 and part not in x_parts(way, d):
-                    continue
-                block = (me if d == 0 else x_block(way, d)) + across
-                arrive(a_part(block, part), as_sems, (way, d, part), sibling)
+                if x_carried(way, d, part) and (d > 0 or way == RIGHT):
+                    arrive(
+                        a_part(x_block(way, d) + across, part), as_sems, (way, d, part), sibling
+                    )
 
     out_width = image_out.shape[1]
     image_sum, text_sum = None, None
@@ -543,44 +575,30 @@
         base = own_columns(tokens[:, window].astype(F32))
         out[...] = (base + gate * total).astype(BF16)
 
-    for copy in started:
-        copy.wait_send()
-
-    def sent(ref, sems, index, device):
-        pltpu.make_async_remote_copy(
-            src_ref=ref,
-            dst_ref=ref,
-            send_sem=sems.at[(0, *index)],
-            recv_sem=sems.at[(1, *index)],
-            device_id=device,
-            device_id_type=MESH,
-        ).wait_send()
+    sent(mod_z.at[pl.ds(0, nz - 1)], modz_sems, (0,), right)
+    sent(mod_all.at[pl.ds(0, heads - 1)], modx_sems, (0,), sibling)
+    blocks = pl.ds(0, nz - 1)
+    sent(weights.at[blocks, pl.ds(0, share), :], w_sems, (0, 0, 0), right)
+    sent(proj_z.at[blocks, :, pl.ds(0, share), :], p_sems, (0, 0, 0), right)
+    sent(proj_all.at[pl.ds(0, heads - 1), :, pl.ds(0, share), :], px_sems, (0,), sibling)
+    sent(key_value.at[blocks], kv_sems, (0, 0, 0), right)
+    sent(attended.at[pl.ds(0, nx - 1)], ax_sems, (0, 0, 0), x_right)
+    sent(attended.at[pl.ds(0, nx)], as_sems, (0, 0, 0), sibling)
+    if paired:
+        sent(weights.at[blocks, pl.ds(0, share), :], wy_sems, (0, 0), partner)
+        sent(all_shares, py_sems, (0,), partner)
 
     def text_sent():
-        for d in range(1, half + 1):
-            for way, to in ((RIGHT, right), (LEFT, left)):
-                for part in parts_at(way, d):
-                    sent(t_part(z, part), t_sems, (way, d, part), to)
+        sent(text_weights.at[blocks], t_sems, (0, 0, 0), right)
         if paired:
-            sent(text_qkv.at[1], tq_sems, (), partner)
+            sent(text_qkv.at[1], tq_sems, (0,), partner)
 
     when_active(text_sent)
     if paired:
 
         @pl.when(jnp.logical_not(active))
         def _():
-            sent(both[0], th_sems, (), partner)
-
-    for i in range(1, heads):
-        block = wrap(me + i, heads)
-        pltpu.make_async_remote_copy(
-            src_ref=proj_z.at[block],
-            dst_ref=proj_all.at[me],
-            send_sem=px_sems.at[0, block],
-            recv_sem=px_sems.at[1, me],
-            device_id=sibling,
-            device_id_type=MESH,
-        ).wait_send()
+            sent(both[0], th_sems, (0,), partner)
 
 
 def solution(mesh):
@@ -613,6 +631,10 @@
         vmem = pl.BlockSpec(memory_space=pltpu.VMEM)
         anywhere = pl.BlockSpec(memory_space=pl.ANY)
         dma = pltpu.SemaphoreType.DMA
+
+        def pair(*shape):
+            return dma((1,)), dma(shape)
+
         return pl.pallas_call(
             functools.partial(kernel, (nz, nx, nc), paired),
             out_shape=(
@@ -647,19 +669,19 @@
                 pltpu.VMEM((local_rows, size), F32),
                 pltpu.VMEM((heads, local_rows, size), BF16),
                 dma((9,)),
-                dma((2, nz)),
-                dma((2, heads)),
-                dma((2, 2, half + 1, 2)),
-                dma((2, 2, half + 1)),
-                dma((2, 2, half + 1, 2)),
-                dma((2,)),
-                dma((2,)),
-                dma((2, 2, half + 1, 2)),
-                dma((2, 2, half + 1)),
-                dma((2, heads)),
-                dma((2, 2, half + 1, 2)),
-                dma((2, 2, nx // 2 + 1, 2)),
-                dma((2, 2, nx // 2 + 1, 2)),
+                *pair(1),
+                *pair(1),
+                *pair(2, half, 2),
+                *pair(2, half),
+                *pair(2, half, 2),
+                *pair(1),
+                *pair(1),
+                *pair(2, half, 2),
+                *pair(1),
+                *pair(1),
+                *pair(2, half, 4),
+                *pair(2, nx // 2, 2),
+                *pair(2, nx // 2 + 1, 2),
             ],
             compiler_params=pltpu.CompilerParams(
                 collective_id=0, has_side_effects=True, vmem_limit_bytes=56 * 1024 * 1024

time: 160 us -> 145 us (0.906)
  Pallas kernels: 154 us -> 140 us
    pallas_call x1, Pallas kernels: 154 us -> 140 us  [body(): pl.pallas_call(functools.partial(kernel, (nz, nx, nc), paired), out_shape...]
where the time goes in v3:
time: 145 us
  Pallas kernels  140 us (97%)
  local copies, waits for them, and re-layouts  2.97 us (2%)
  between operations  1.93 us (1%)
    pallas_call x1, Pallas kernels, body(): pl.pallas_call(functools.partial(kernel, (nz, nx, nc), paired), out_shape...  140 us

profile of v3, /device:TPU:65, one launch (start us, length us, event | category | flops | bytes accessed | tf_op | source)
XLA Modules:
  0.0 145.2 jit_solution(13524261923920354770)
XLA Ops:
  1.9 140.3 %shard_map.122 = (bf16[256,192]{1,0:T(8,128)(2,1)}, bf16[32,192]{1,0:T(8,128)(2,1)}) custom-call(s32[1]{0:T(128)S(6)} %copy.16.text_length, s32[1]{0:T(128)S(6)} %copy.15.timestep, bf16[256,3072]{1,0:T(8,128)(2,1)} %image_hbm.1, bf16[32,3072]{1,0:T(8,128)(2,1)} %text_hbm.1, bf16[50,3072]{1,0:T(8,128)(2,1)} %table_hbm.1, bf16[192,1152]{1,0:T(8,128)(2,1)} %mod_hbm.1, ...), custom_call_target="tpu_custom_call" | custom-call | tf_op jit(solution)/shard_map/pallas_call | solution.py:638
  142.3 1.6 %copy.13 = bf16[256,192]{0,1:T(8,128)(2,1)} copy(bf16[256,192]{1,0:T(8,128)(2,1)} %get-tuple-element.2) | data formatting | bytes 196608 | tf_op jit(solution)/shard_map/pallas_call | solution.py:638
  143.9 1.3 copy.17

commit v4 on v3

--- a/solution.py
+++ b/solution.py
@@ -24,8 +24,8 @@
 def kernel(
     sizes,
     paired,
-    text_length,
-    timestep,
+    length_hbm,
+    step_hbm,
     image_hbm,
     text_hbm,
     table_hbm,
@@ -42,7 +42,8 @@
     time_table,
     mod_weight,
     norm_gain,
-    mod_z,
+    mod_rows,
+    mod_in,
     mod_all,
     mean_of,
     rstd_of,
@@ -61,12 +62,14 @@
     row_sum,
     mixed,
     attended,
+    text_length,
+    timestep,
     load_sem,
+    mod_sems,
     *pairs,
 ):
     nz, nx, nc = sizes
     (
-        modz_sems,
         modx_sems,
         w_sems,
         wy_sems,
@@ -144,10 +147,12 @@
         pltpu.make_async_copy(src, dst, load_sem.at[i])
         for i, (src, dst) in enumerate(
             (
+                (step_hbm, timestep),
+                (length_hbm, text_length),
                 (table_hbm.at[:, table_window], time_table),
                 (mod_hbm, mod_weight),
-                (qkv_image, weights.at[z]),
-                (qkv_text, text_weights.at[z]),
+                (qkv_image, weights.at[rows_at(z * slab, slab), :]),
+                (qkv_text, text_weights.at[rows_at(z * slab, slab), :]),
                 (proj_image, proj_z.at[z, 0]),
                 (proj_text, proj_z.at[z, 1]),
                 (text_hbm, text_tokens),
@@ -158,7 +163,7 @@
     ]
     for copy in loads:
         copy.start()
-    for copy in loads[:6]:
+    for copy in loads[:8]:
         copy.wait()
 
     picked = lax.broadcasted_iota(jnp.int32, time_table.shape, 0) == timestep[0]
@@ -167,7 +172,10 @@
     )
     vector = (embedded / (1.0 + jnp.exp(-embedded))).astype(BF16)
     vector_rows = jnp.where(lax.rem(z, 2) == 0, vector[:, :slab], vector[:, slab:])
-    mod_z[z] = jnp.dot(vector_rows, mod_weight[...], preferred_element_type=F32)
+    partial_sum = jnp.dot(vector_rows, mod_weight[...], preferred_element_type=F32)
+    chunks = partial_sum.shape[1] // 128
+    for i in range(chunks):
+        mod_rows[i] = partial_sum[:, i * 128 : (i + 1) * 128]
 
     chunk = 16
 
@@ -186,8 +194,60 @@
 
     pl.semaphore_wait(barrier, len(greeted))
 
-    for i in range(1, nz):
-        send(mod_z.at[z], mod_z.at[z], modz_sems, (0,), peers[i - 1])
+    def is_owner(i):
+        return z == i % nz
+
+    def mod_copy(i, src, dst, stage, device):
+        return pltpu.make_async_remote_copy(
+            src_ref=src,
+            dst_ref=dst,
+            send_sem=mod_sems.at[0, stage, i],
+            recv_sem=mod_sems.at[1, stage, i],
+            device_id=device,
+            device_id_type=MESH,
+        )
+
+    def mod_total(i):
+        return mod_all.at[me, :, pl.ds(i * 128, 128)]
+
+    def mod_partial():
+        for i in range(chunks):
+
+            @pl.when(jnp.logical_not(is_owner(i)))
+            def _():
+                mod_copy(i, mod_rows.at[i], mod_in.at[i, z], 0, {"seq": i % nz}).start()
+
+            @pl.when(is_owner(i))
+            def _():
+                mod_in[i, z] = mod_rows[i]
+
+    def mod_reduce():
+        for i in range(chunks):
+            others = mod_in.at[i, pl.ds(0, nz - 1)]
+
+            @pl.when(is_owner(i))
+            def _():
+                mod_copy(i, others, others, 0, right).wait_recv()
+                total = mod_in[i, 0]
+                for k in range(1, nz):
+                    total = total + mod_in[i, k]
+                mod_all[me, :, i * 128 : (i + 1) * 128] = total
+                for device in peers:
+                    mod_copy(i, mod_total(i), mod_total(i), 1, device).start()
+
+    def mod_sent():
+        for i in range(chunks):
+            others = mod_in.at[i, pl.ds(0, nz - 1)]
+
+            @pl.when(jnp.logical_not(is_owner(i)))
+            def _():
+                mod_copy(i, mod_rows.at[i], mod_rows.at[i], 0, right).wait_send()
+
+            @pl.when(is_owner(i))
+            def _():
+                mod_copy(i, others, others, 1, right).wait_send()
+
+    mod_partial()
 
     half = nz // 2
 
@@ -210,13 +270,14 @@
     share = slab // 2 if paired else slab
 
     def w_part(block, part):
-        return weights.at[block, rows_at(own * share + part * (share // 2), share // 2), :]
+        start = block * slab + own * share + part * (share // 2)
+        return weights.at[rows_at(start, share // 2), :]
 
     def w_share(block, of):
-        return weights.at[block, rows_at(of * share, share), :]
+        return weights.at[rows_at(block * slab + of * share, share), :]
 
     def t_part(block, part):
-        return text_weights.at[block, pl.ds(part * (slab // 2), slab // 2), :]
+        return text_weights.at[rows_at(block * slab + part * (slab // 2), slab // 2), :]
 
     def p_part(block, part):
         return proj_z.at[block, :, rows_at(own * share + part * (share // 2), share // 2), :]
@@ -247,17 +308,18 @@
 
     weight_step(0)
 
-    for copy in loads[6:]:
+    for copy in loads[8:]:
         copy.wait()
     statistics(text_tokens, 0, text_rows, image_rows)
     statistics(image_tokens, 0, image_rows // 2, 0)
 
     def mod_over_seq():
-        arrive(mod_z.at[pl.ds(0, nz - 1)], modz_sems, (0,), right)
-        total = mod_z[0]
-        for i in range(1, nz):
-            total = total + mod_z[i]
-        mod_all[me] = total
+        for i in range(chunks):
+
+            @pl.when(jnp.logical_not(is_owner(i)))
+            def _():
+                mod_copy(i, mod_total(i), mod_total(i), 1, right).wait_recv()
+
         for device in plane:
             send(mod_all.at[me], mod_all.at[me], modx_sems, (0,), device)
 
@@ -283,26 +345,26 @@
                 scaling = mod_piece((stream * 3 + 1) * pieces + p)
                 values = tokens[rows, p * piece : (p + 1) * piece].astype(F32)
                 values = ((values - center) * scale * (1.0 + scaling) + shift).astype(BF16)
-                hidden[2 * p, rows, :] = values[:, :slab]
-                hidden[2 * p + 1, rows, :] = values[:, slab:]
+                hidden[rows, p * piece : (p + 1) * piece] = values
             return carry
 
         lax.fori_loop(first // chunk, last // chunk, one, 0)
 
-    sum_image[...] = jnp.zeros_like(sum_image)
-    sum_text[...] = jnp.zeros_like(sum_text)
+    depth = 4 * slab
 
     def block_at(j):
         step = lax.div(j + 1, 2)
         return wrap(jnp.where(lax.rem(j, 2) == 1, z - step, z + step), nz)
 
-    def project(hidden, total, shards, first, last):
-        def one(j, carry):
-            block = block_at(j)
-            total[...] += jnp.dot(hidden[block], shards[block], preferred_element_type=F32)
+    def project(hidden, total, shards):
+        total[...] = jnp.zeros_like(total)
+
+        def one(i, carry):
+            at = pl.ds(pl.multiple_of(i * depth, 128), depth)
+            total[...] += jnp.dot(hidden[:, at], shards[at, :], preferred_element_type=F32)
             return carry
 
-        lax.fori_loop(first, last, one, 0)
+        lax.fori_loop(0, nz * slab // depth, one, 0)
 
     def give_block(block):
         target = {"tensor": lax.div(block, nc), "sub": lax.rem(block, nc)}
@@ -354,18 +416,10 @@
                 send(both[0], both[1], th_sems, (0,), partner)
 
     both = (
-        hidden_text.at[:, pl.ds(0, text_rows), :],
-        hidden_text.at[:, pl.ds(text_rows, text_rows), :],
+        hidden_text.at[pl.ds(0, text_rows), :],
+        hidden_text.at[pl.ds(text_rows, text_rows), :],
     )
     middle = image_rows // 2
-
-    def project_all(first, last):
-        project(hidden_image, sum_image, weights, first, last)
-        when_active(lambda: project(hidden_text, sum_text, text_weights, first, last))
-
-    def receive_hidden():
-        if paired:
-            when_active(lambda: arrive(both[1], th_sems, (0,), partner))
 
     def stats_of(first):
         return lambda: statistics(image_tokens, first, first + middle // 2, 0)
@@ -378,30 +432,18 @@
         hide(text_tokens, hidden_text, 1, 0, text_rows, image_rows)
         hidden_exchange()
 
-    done = 0
-
-    def multiply(until):
-        def run():
-            nonlocal done
-            project_all(done, until)
-            done = max(done, until)
-
-        return run
-
     quarter_rows = middle // 2
     early = [
         (1, 0, stats_of(middle)),
         (1, 1, stats_of(middle + quarter_rows)),
-        (2, 1, mod_over_seq),
-        (4, 0, hide_text),
-        (4, 1, hide_of(0)),
-        (5, 0, hide_of(quarter_rows)),
-        (5, 1, hide_of(middle)),
-        (6, 0, hide_of(middle + quarter_rows)),
-        (6, 0, receive_hidden),
+        (2, 1, mod_reduce),
+        (4, 1, mod_over_seq),
+        (6, 0, hide_text),
+        (6, 1, hide_of(0)),
+        (7, 0, hide_of(quarter_rows)),
+        (7, 1, hide_of(middle)),
+        (8, 1, hide_of(middle + quarter_rows)),
     ]
-    if half >= 8:
-        early += [(6, 1, multiply(3)), (7, 0, multiply(6)), (7, 1, multiply(9)), (8, 0, multiply(11))]
     for d in range(1, half + 1):
         tasks = [
             [task for at, place, task in early if (min(at, half), place if at < half else 1) == (d, p)]
@@ -415,7 +457,7 @@
             weight_wait(d - 2)
     for d in range(max(1, half - 1), half + 1):
         weight_wait(d)
-        multiply(min(2 * d + 1, nz))()
+    project(hidden_image, sum_image, weights)
 
     def normed(values, gain):
         return (
@@ -445,6 +487,9 @@
         ring_part(0, part, 4, kv_part, kv_sems)
 
     def text_projection():
+        if paired:
+            arrive(both[1], th_sems, (0,), partner)
+        project(hidden_text, sum_text, text_weights)
         for side in (0, 1) if paired else (0,):
             parts = normed_three(sum_text[side * text_rows : (side + 1) * text_rows, :], 1)
             for i in range(3):
@@ -549,7 +594,7 @@
                         a_part(x_block(way, d) + across, part), as_sems, (way, d, part), sibling
                     )
 
-    out_width = image_out.shape[1]
+    out_width = text_out.shape[1]
     image_sum, text_sum = None, None
     for h in range(0, heads, 2):
         rows = jnp.concatenate([attended[h], attended[h + 1]], axis=1)
@@ -573,23 +618,24 @@
     ):
         gate = own_columns(mod_piece((stream * 3 + 2) * pieces + x))
         base = own_columns(tokens[:, window].astype(F32))
-        out[...] = (base + gate * total).astype(BF16)
-
-    sent(mod_z.at[pl.ds(0, nz - 1)], modz_sems, (0,), right)
+        result = base + gate * total
+        out[...] = (jnp.transpose(result) if stream == 0 else result).astype(BF16)
+
+    mod_sent()
     sent(mod_all.at[pl.ds(0, heads - 1)], modx_sems, (0,), sibling)
     blocks = pl.ds(0, nz - 1)
-    sent(weights.at[blocks, pl.ds(0, share), :], w_sems, (0, 0, 0), right)
+    sent(weights.at[pl.ds(0, (nz - 1) * share), :], w_sems, (0, 0, 0), right)
     sent(proj_z.at[blocks, :, pl.ds(0, share), :], p_sems, (0, 0, 0), right)
     sent(proj_all.at[pl.ds(0, heads - 1), :, pl.ds(0, share), :], px_sems, (0,), sibling)
     sent(key_value.at[blocks], kv_sems, (0, 0, 0), right)
     sent(attended.at[pl.ds(0, nx - 1)], ax_sems, (0, 0, 0), x_right)
     sent(attended.at[pl.ds(0, nx)], as_sems, (0, 0, 0), sibling)
     if paired:
-        sent(weights.at[blocks, pl.ds(0, share), :], wy_sems, (0, 0), partner)
+        sent(weights.at[pl.ds(0, (nz - 1) * share), :], wy_sems, (0, 0), partner)
         sent(all_shares, py_sems, (0,), partner)
 
     def text_sent():
-        sent(text_weights.at[blocks], t_sems, (0, 0, 0), right)
+        sent(text_weights.at[pl.ds(0, (nz - 1) * slab), :], t_sems, (0, 0, 0), right)
         if paired:
             sent(text_qkv.at[1], tq_sems, (0,), partner)
 
@@ -599,6 +645,11 @@
         @pl.when(jnp.logical_not(active))
         def _():
             sent(both[0], th_sems, (0,), partner)
+
+
+def hand_out(image, text, image_out, text_out):
+    image_out[...] = image[...]
+    text_out[...] = text[...]
 
 
 def solution(mesh):
@@ -635,13 +686,13 @@
         def pair(*shape):
             return dma((1,)), dma(shape)
 
-        return pl.pallas_call(
+        results = pl.pallas_call(
             functools.partial(kernel, (nz, nx, nc), paired),
             out_shape=(
-                jax.ShapeDtypeStruct((image_rows, out_width), BF16),
+                jax.ShapeDtypeStruct((out_width, image_rows), BF16),
                 jax.ShapeDtypeStruct((text_rows, out_width), BF16),
             ),
-            in_specs=[pl.BlockSpec(memory_space=pltpu.SMEM)] * 2 + [anywhere] * 9,
+            in_specs=[pl.BlockSpec(memory_space=pltpu.HBM)] * 2 + [anywhere] * 9,
             out_specs=(vmem, vmem),
             scratch_shapes=[
                 pltpu.VMEM(image_tokens.shape, BF16),
@@ -649,14 +700,15 @@
                 pltpu.VMEM((time_table.shape[0], 2 * slab), BF16),
                 pltpu.VMEM(mod_weight.shape, BF16),
                 pltpu.VMEM(gains.shape, F32),
-                pltpu.VMEM((nz, 1, mod_weight.shape[1]), F32),
+                pltpu.VMEM((mod_weight.shape[1] // 128, 1, 128), F32),
+                pltpu.VMEM((mod_weight.shape[1] // 128, nz, 1, 128), F32),
                 pltpu.VMEM((heads, 1, mod_weight.shape[1]), F32),
                 pltpu.VMEM((local_rows, 128), F32),
                 pltpu.VMEM((local_rows, 128), F32),
-                pltpu.VMEM((nz, image_rows, slab), BF16),
-                pltpu.VMEM((nz, 2 * text_rows, slab), BF16),
-                pltpu.VMEM((nz, slab, columns), BF16),
-                pltpu.VMEM((nz, slab, columns), BF16),
+                pltpu.VMEM((image_rows, width), BF16),
+                pltpu.VMEM((2 * text_rows, width), BF16),
+                pltpu.VMEM((width, columns), BF16),
+                pltpu.VMEM((width, columns), BF16),
                 pltpu.VMEM((image_rows, columns), F32),
                 pltpu.VMEM((2 * text_rows, columns), F32),
                 pltpu.VMEM((2, text_rows, columns), BF16),
@@ -668,8 +720,10 @@
                 pltpu.VMEM((local_rows, 128), F32),
                 pltpu.VMEM((local_rows, size), F32),
                 pltpu.VMEM((heads, local_rows, size), BF16),
-                dma((9,)),
-                *pair(1),
+                pltpu.SMEM((1,), jnp.int32),
+                pltpu.SMEM((1,), jnp.int32),
+                dma((11,)),
+                dma((2, 2, mod_weight.shape[1] // 128)),
                 *pair(1),
                 *pair(2, half, 2),
                 *pair(2, half),
@@ -699,6 +753,13 @@
             proj_image.T,
             proj_text.T,
         )
+        image_turned, text_out = pl.pallas_call(
+            hand_out,
+            out_shape=tuple(jax.ShapeDtypeStruct(r.shape, r.dtype) for r in results),
+            in_specs=[vmem] * 2,
+            out_specs=(vmem, vmem),
+        )(*results)
+        return image_turned.T, text_out
 
     return jax.shard_map(
         body,

time: 145 us -> 143 us (0.986)
  local copies, waits for them, and re-layouts: 2.97 us -> 0 us
    pallas_call x1 -> x0, local copies, waits for them, and re-layouts: 1.65 us -> none  [body(): pl.pallas_call(functools.partial(kernel, (nz, nx, nc), paired), out_shape...]
    pallas_call x0 -> x1, Pallas kernels: none -> 1.55 us  [body(): pl.pallas_call(hand_out, out_shape=tuple((jax.ShapeDtypeStruct(r.shape, r...]
where the time goes in v4:
time: 143 us
  Pallas kernels  141 us (99%)
  between operations  1.93 us (1%)
    pallas_call x1, Pallas kernels, body(): pl.pallas_call(functools.partial(kernel, (nz, nx, nc), paired), out_shape...  140 us

profile of v4, /device:TPU:65, one launch (start us, length us, event | category | flops | bytes accessed | tf_op | source)
XLA Modules:
  0.0 143.1 jit_solution(10908458648231789373)
XLA Ops:
  1.9 139.6 %shard_map.122 = (bf16[192,256]{1,0:T(8,128)(2,1)}, bf16[32,192]{1,0:T(8,128)(2,1)}) custom-call(s32[1]{0:T(128)S(6)} %copy.14.length_hbm, s32[1]{0:T(128)S(6)} %copy.13.step_hbm, bf16[256,3072]{1,0:T(8,128)(2,1)} %image_hbm.1, bf16[32,3072]{1,0:T(8,128)(2,1)} %text_hbm.1, bf16[50,3072]{1,0:T(8,128)(2,1)} %table_hbm.1, bf16[192,1152]{1,0:T(8,128)(2,1)} %mod_hbm.1, ...), custom_call_target="tpu_custom_call" | custom-call | tf_op jit(solution)/shard_map/pallas_call | solution.py:689
  141.5 1.5 %shard_map.123 = (bf16[192,256]{1,0:T(8,128)(2,1)}, bf16[32,192]{1,0:T(8,128)(2,1)}) custom-call(bf16[192,256]{1,0:T(8,128)(2,1)} %get-tuple-element.6.image, bf16[32,192]{1,0:T(8,128)(2,1)} %get-tuple-element.7.text), custom_call_target="tpu_custom_call" | custom-call | tf_op jit(solution)/shard_map/pallas_call | solution.py:756

commit v5 on v4

--- a/solution.py
+++ b/solution.py
@@ -137,7 +137,8 @@
         {"tensor": lax.div(wrap(me + i, heads), nc), "sub": lax.rem(wrap(me + i, heads), nc)}
         for i in range(1, heads)
     ]
-    greeted = peers + plane + ([partner] if paired else [])
+    far_first = sorted(range(1, nz), key=lambda i: -min(i, nz - i))
+    greeted = [peers[i - 1] for i in far_first] + plane + ([partner] if paired else [])
     for device in greeted:
         pl.semaphore_signal(barrier, inc=1, device_id=device, device_id_type=MESH)
 
@@ -273,8 +274,9 @@
         start = block * slab + own * share + part * (share // 2)
         return weights.at[rows_at(start, share // 2), :]
 
-    def w_share(block, of):
-        return weights.at[rows_at(block * slab + of * share, share), :]
+    def y_part(block, part, of):
+        start = block * slab + of * share + part * (share // 2)
+        return weights.at[rows_at(start, share // 2), :]
 
     def t_part(block, part):
         return text_weights.at[rows_at(block * slab + part * (slab // 2), slab // 2), :]
@@ -288,23 +290,22 @@
     def weight_step(d, tasks=((), ())):
         for part in (0, 1):
             ring_part(d, part, 2, w_part, w_sems)
+            if paired and d > 0:
+                for way in (RIGHT, LEFT):
+                    if carried(way, d, part, 2):
+                        here = y_part(slab_of(way, d), part, own)
+                        send(here, here, wy_sems, (way, d - 1, part), partner)
             when_active(lambda: ring_part(d, part, 2, t_part, t_sems))
-            if part == 0:
-                for task in tasks[0]:
-                    task()
-        if paired and d > 0:
-            for way in (RIGHT, LEFT):
-                if way == RIGHT or d < half:
-                    here = w_share(slab_of(way, d), own)
-                    send(here, here, wy_sems, (way, d - 1), partner)
-        for task in tasks[1]:
-            task()
+            for task in tasks[part]:
+                task()
 
     def weight_wait(d):
         if paired:
-            for way in (RIGHT, LEFT):
-                if way == RIGHT or d < half:
-                    arrive(w_share(slab_of(way, d), 1 - own), wy_sems, (way, d - 1), partner)
+            for part in (0, 1):
+                for way in (RIGHT, LEFT):
+                    if carried(way, d, part, 2):
+                        here = y_part(slab_of(way, d), part, 1 - own)
+                        arrive(here, wy_sems, (way, d - 1, part), partner)
 
     weight_step(0)
 
@@ -350,21 +351,24 @@
 
         lax.fori_loop(first // chunk, last // chunk, one, 0)
 
+    sum_image[...] = jnp.zeros_like(sum_image)
+    sum_text[...] = jnp.zeros_like(sum_text)
     depth = 4 * slab
 
     def block_at(j):
         step = lax.div(j + 1, 2)
         return wrap(jnp.where(lax.rem(j, 2) == 1, z - step, z + step), nz)
 
-    def project(hidden, total, shards):
-        total[...] = jnp.zeros_like(total)
-
-        def one(i, carry):
-            at = pl.ds(pl.multiple_of(i * depth, 128), depth)
+    pieces_of_depth = nz * slab // depth
+    first_piece = lax.div(z * slab, depth)
+    order = [i for i in range(pieces_of_depth) if i != pieces_of_depth // 2]
+    order += [pieces_of_depth // 2]
+
+    def project(hidden, total, shards, which):
+        for i in which:
+            index = lax.rem(first_piece + i, pieces_of_depth)
+            at = pl.ds(pl.multiple_of(index * depth, 128), depth)
             total[...] += jnp.dot(hidden[:, at], shards[at, :], preferred_element_type=F32)
-            return carry
-
-        lax.fori_loop(0, nz * slab // depth, one, 0)
 
     def give_block(block):
         target = {"tensor": lax.div(block, nc), "sub": lax.rem(block, nc)}
@@ -455,9 +459,11 @@
         proj_advance(d)
         if d > 2:
             weight_wait(d - 2)
-    for d in range(max(1, half - 1), half + 1):
-        weight_wait(d)
-    project(hidden_image, sum_image, weights)
+    if half > 1:
+        weight_wait(half - 1)
+    project(hidden_image, sum_image, weights, order[:-1])
+    weight_wait(half)
+    project(hidden_image, sum_image, weights, order[-1:])
 
     def normed(values, gain):
         return (
@@ -489,7 +495,7 @@
     def text_projection():
         if paired:
             arrive(both[1], th_sems, (0,), partner)
-        project(hidden_text, sum_text, text_weights)
+        project(hidden_text, sum_text, text_weights, order)
         for side in (0, 1) if paired else (0,):
             parts = normed_three(sum_text[side * text_rows : (side + 1) * text_rows, :], 1)
             for i in range(3):
@@ -631,7 +637,7 @@
     sent(attended.at[pl.ds(0, nx - 1)], ax_sems, (0, 0, 0), x_right)
     sent(attended.at[pl.ds(0, nx)], as_sems, (0, 0, 0), sibling)
     if paired:
-        sent(weights.at[pl.ds(0, (nz - 1) * share), :], wy_sems, (0, 0), partner)
+        sent(weights.at[pl.ds(0, (nz - 1) * share), :], wy_sems, (0, 0, 0), partner)
         sent(all_shares, py_sems, (0,), partner)
 
     def text_sent():
@@ -726,7 +732,7 @@
                 dma((2, 2, mod_weight.shape[1] // 128)),
                 *pair(1),
                 *pair(2, half, 2),
-                *pair(2, half),
+                *pair(2, half, 2),
                 *pair(2, half, 2),
                 *pair(1),
                 *pair(1),

time: 143 us -> 141 us (0.986)
  Pallas kernels: 141 us -> 139 us
    pallas_call x1, Pallas kernels: 140 us -> 137 us  [body(): pl.pallas_call(functools.partial(kernel, (nz, nx, nc), paired), out_shape...]
where the time goes in v5:
time: 141 us; the launch traced here: 140 us
  Pallas kernels  139 us (99%)
  between operations  1.93 us (1%)
    pallas_call x1, Pallas kernels, body(): pl.pallas_call(functools.partial(kernel, (nz, nx, nc), paired), out_shape...  137 us

profile of v5, /device:TPU:65, one launch (start us, length us, event | category | flops | bytes accessed | tf_op | source)
XLA Modules:
  0.0 140.5 jit_solution(7269287868473827330)
XLA Ops:
  1.9 137.0 %shard_map.122 = (bf16[192,256]{1,0:T(8,128)(2,1)}, bf16[32,192]{1,0:T(8,128)(2,1)}) custom-call(s32[1]{0:T(128)S(6)} %copy.14.length_hbm, s32[1]{0:T(128)S(6)} %copy.13.step_hbm, bf16[256,3072]{1,0:T(8,128)(2,1)} %image_hbm.1, bf16[32,3072]{1,0:T(8,128)(2,1)} %text_hbm.1, bf16[50,3072]{1,0:T(8,128)(2,1)} %table_hbm.1, bf16[192,1152]{1,0:T(8,128)(2,1)} %mod_hbm.1, ...), custom_call_target="tpu_custom_call" | custom-call | tf_op jit(solution)/shard_map/pallas_call | solution.py:695
  139.0 1.5 %shard_map.123 = (bf16[192,256]{1,0:T(8,128)(2,1)}, bf16[32,192]{1,0:T(8,128)(2,1)}) custom-call(bf16[192,256]{1,0:T(8,128)(2,1)} %get-tuple-element.6.image, bf16[32,192]{1,0:T(8,128)(2,1)} %get-tuple-element.7.text), custom_call_target="tpu_custom_call" | custom-call | tf_op jit(solution)/shard_map/pallas_call | solution.py:762

commit v6 on v5

--- a/solution.py
+++ b/solution.py
@@ -564,19 +564,18 @@
 
     x_half = nx // 2
     x_right, x_left = {"tensor": wrap(x + 1, nx)}, {"tensor": wrap(x - 1, nx)}
-    half_rows = local_rows // 2
 
     def x_carried(way, d, part):
-        return d < x_half or (part == 0) == (way == RIGHT)
+        return d < x_half or (part < 2) == (way == RIGHT)
 
     def x_block(way, d):
         return (wrap(x - d, nx) if way == RIGHT else wrap(x + d, nx)) * nc + c
 
     def a_part(block, part):
-        return attended.at[block, pl.ds(part * half_rows, half_rows), :]
+        return attended.at[block, pl.ds(starts[part], starts[part + 1] - starts[part]), :]
 
     for d in range(0, x_half + 1):
-        for part in (0, 1):
+        for part in range(4):
             for way, to in ((RIGHT, x_right), (LEFT, x_left)):
                 if not x_carried(way, d, part):
                     continue
@@ -593,7 +592,7 @@
 
     across = 1 - 2 * c
     for d in range(0, x_half + 1):
-        for part in (0, 1):
+        for part in range(4):
             for way in (RIGHT, LEFT):
                 if x_carried(way, d, part) and (d > 0 or way == RIGHT):
                     arrive(
@@ -740,8 +739,8 @@
                 *pair(1),
                 *pair(1),
                 *pair(2, half, 4),
-                *pair(2, nx // 2, 2),
-                *pair(2, nx // 2 + 1, 2),
+                *pair(2, nx // 2, 4),
+                *pair(2, nx // 2 + 1, 4),
             ],
             compiler_params=pltpu.CompilerParams(
                 collective_id=0, has_side_effects=True, vmem_limit_bytes=56 * 1024 * 1024

time: 141 us -> 141 us (level)
  no operation moved by 1% of the time
where the time goes in v6:
time: 141 us
  Pallas kernels  139 us (99%)
  between operations  1.93 us (1%)
    pallas_call x1, Pallas kernels, body(): pl.pallas_call(functools.partial(kernel, (nz, nx, nc), paired), out_shape...  137 us

profile of v6, /device:TPU:65, one launch (start us, length us, event | category | flops | bytes accessed | tf_op | source)
XLA Modules:
  0.0 140.5 jit_solution(7736975291215621277)
XLA Ops:
  1.9 137.0 %shard_map.122 = (bf16[192,256]{1,0:T(8,128)(2,1)}, bf16[32,192]{1,0:T(8,128)(2,1)}) custom-call(s32[1]{0:T(128)S(6)} %copy.14.length_hbm, s32[1]{0:T(128)S(6)} %copy.13.step_hbm, bf16[256,3072]{1,0:T(8,128)(2,1)} %image_hbm.1, bf16[32,3072]{1,0:T(8,128)(2,1)} %text_hbm.1, bf16[50,3072]{1,0:T(8,128)(2,1)} %table_hbm.1, bf16[192,1152]{1,0:T(8,128)(2,1)} %mod_hbm.1, ...), custom_call_target="tpu_custom_call" | custom-call | tf_op jit(solution)/shard_map/pallas_call | solution.py:694
  139.0 1.5 %shard_map.123 = (bf16[192,256]{1,0:T(8,128)(2,1)}, bf16[32,192]{1,0:T(8,128)(2,1)}) custom-call(bf16[192,256]{1,0:T(8,128)(2,1)} %get-tuple-element.6.image, bf16[32,192]{1,0:T(8,128)(2,1)} %get-tuple-element.7.text), custom_call_target="tpu_custom_call" | custom-call | tf_op jit(solution)/shard_map/pallas_call | solution.py:761
